TPU v7x, 128 devices: a whole 4x4x4 slice. The times are simulated.
128 devices in a mesh: pair: 8 (over x, core), row: 16 (over z, y).
Axes of the slice: x: 4, y: 4, z: 4, core: 2. Of those that a mesh axis runs over, the one named last changes fastest.
Arguments:
- descriptors: bfloat16 [64, 2048, 256], P('pair', 'row'), parts along dimension 0, may hold values from -8 to 8
- counts: int32 [64], P('pair'), parts along dimension 0, may hold values from 512 to 2048
- pairs: int32 [32, 2], P('pair'), parts along dimension 0, may hold values from 0 to 7, as said below
- bin_score: float32 [1], replicated, may hold values from 0.5 to 2
Outputs:
- log_match: float32 [32, 2048, 2048], P('pair', 'row'), parts along dimension 0
- row_bins: float32 [32, 2048], P('pair', 'row'), parts along dimension 0
- col_bins: float32 [32, 2048], P('pair'), parts along dimension 0
There are 8 independent parts, one for each index of `pair`. A program takes and returns all parts, laid end to end along the dimension named above; an argument that names none is the same for every part. Nothing has to cross between parts.
Inputs may be any that keep to these rules, and one draw needn't show every extreme that they name: Image k's keypoints are its first counts[k] slots. `pairs`: the two images of a pair differ.
All inputs are finite; a program needn't handle non-finite values.
Results may differ from a plain program's by a relative error of at most 0.0003.
Values may be sent and summed in bfloat16 or wider, within the bound.
No kernel may reach another device: no remote copies, remote signals or barrier semaphores. Data moves between devices by JAX's collectives and lax.ppermute only.
A program may use at most 64 MiB of HBM per device.

v0:
```python
import functools

import jax
import jax.numpy as jnp
from jax import lax
from jax.experimental import pallas as pl
from jax.experimental.pallas import tpu as pltpu
from jax.sharding import Mesh
from jax.sharding import PartitionSpec as P


ITERS = 10
KP = 2048
D = 256
BLK = 128
NBLK = KP // BLK
NCH = KP // 128
BIAS = 40.0
BIG = 256
SHARE = 8
AXES = ("pair", "row_0", "row_1")


def tree_sum(terms):
    while len(terms) > 1:
        pairs = [terms[k] + terms[k + 1] for k in range(0, len(terms) - 1, 2)]
        terms = pairs + ([terms[-1]] if len(terms) % 2 else [])
    return terms[0]


def sinkhorn_kernel(
    params, bins, x0, x1, x2, x3, out,
    kern, raw_0, raw_1, rows, cols, part, peak, wide_a, wide_mu, bin_hot, scale_b, share_b, sems,
):
    n_rows = params[4]
    n_cols = params[8]
    alpha = bins[0]
    copies = []
    for k, x in enumerate((x0, x1, x2, x3)):
        for t in range(4):
            spot = pl.ds(pl.multiple_of(block_at(params, k, t) * BLK, BLK), BLK)
            for side, target in ((1, cols), (0, rows)):
                copy = pltpu.make_async_copy(x.at[t, side], target.at[spot], sems.at[k, t, side])
                copy.start()
                copies.append(copy)
    lanes = lax.broadcasted_iota(jnp.int32, (1, 128), 1)
    row_count = jnp.full((8, 128), n_rows.astype(jnp.float32))
    col_count = jnp.full((8, 128), n_cols.astype(jnp.float32))
    mu = 1.0 / (row_count + col_count)
    mu_bin = col_count * mu
    nu_bin = row_count * mu
    for c in range(NCH):
        kept = jnp.broadcast_to(lanes + c * 128 < n_cols, (8, 128))
        scale_b[:, pl.ds(c * 128, 128)] = jnp.where(kept, 1.0, 0.0)
        share_b[:, pl.ds(c * 128, 128)] = jnp.where(kept, mu, 0.0)
    out[...] = jnp.zeros_like(out)
    pair_rows = 2 * BIG
    steps = (n_rows + pair_rows - 1) // pair_rows
    for copy in copies:
        copy.wait()

    @pl.loop(0, NBLK)
    def _(c):
        spot = pl.ds(pl.multiple_of(c * BLK, BLK), BLK)
        place = c * BLK + lax.broadcasted_iota(jnp.int32, (BLK, D), 0)
        kept = jnp.where(place < n_cols, 1.0, 0.0)
        cols[spot, :] = (cols[spot, :].astype(jnp.float32) * kept).astype(jnp.bfloat16)
        for g in range(0, BLK, 8):
            at = pl.ds(pl.multiple_of(c * BLK + g, 8), 8)
            row = c * BLK + g + lax.broadcasted_iota(jnp.int32, (8, 128), 0)
            wide_mu[at, :] = jnp.where(row < n_rows, mu, 0.0)

    def block(r):
        return pl.multiple_of(r * BIG, BIG)

    def scores_of(r, raw):
        left = rows[pl.ds(block(r), BIG), :] * jnp.bfloat16(0.0625)
        for c in range(NCH // 2):
            raw[:, pl.ds(c * 256, 256)] = lax.dot_general(
                left,
                cols[pl.ds(c * 256, 256), :],
                (((1,), (1,)), ((), ())),
                preferred_element_type=jnp.float32,
            )

    def exps_of(r, raw):
        base = block(r)
        for g in range(0, BIG, 8):
            at, near = pl.ds(base + g, 8), pl.ds(g, 8)
            tops = [raw[near, pl.ds(c * 128, 128)] for c in range(NCH)]
            while len(tops) > 1:
                tops = [jnp.maximum(tops[k], tops[k + 1]) for k in range(0, len(tops), 2)]
            drop = jnp.maximum(jnp.max(tops[0], axis=1, keepdims=True), alpha) - BIAS
            peak[at, :] = jnp.broadcast_to(drop, (8, 128))
        for g in range(0, BIG, 8):
            at, near = pl.ds(base + g, 8), pl.ds(g, 8)
            drop = peak[at, :]
            for c in range(NCH):
                ch = pl.ds(c * 128, 128)
                kern[at, ch] = jnp.exp(raw[near, ch] - drop)
            bin_hot[at, :] = jnp.where(lanes == 0, jnp.exp(alpha - drop), 0.0)

    scores_of(0, raw_0)

    @pl.loop(0, steps - 1)
    def _(m):
        scores_of(2 * m + 1, raw_1)
        exps_of(2 * m, raw_0)
        scores_of(2 * m + 2, raw_0)
        exps_of(2 * m + 1, raw_1)

    scores_of(2 * steps - 1, raw_1)
    exps_of(2 * steps - 2, raw_0)
    exps_of(2 * steps - 1, raw_1)

    def sums(r, bin_b, low):
        base = block(r)
        for q in range(0, BIG // 8, SHARE):
            sets = [pl.ds(base + 8 * (q + g), 8) for g in range(SHARE)]
            acc = [bin_hot[sets[g], :] * bin_b for g in range(SHARE)]
            for c in range(NCH):
                ch = pl.ds(c * 128, 128)
                b = scale_b[:, ch]
                for g in range(SHARE):
                    acc[g] = acc[g] + kern[sets[g], ch] * b
            for g in range(SHARE):
                part[pl.ds(low + 8 * (q + g), 8), :] = acc[g]

    def scales(r, low):
        base = block(r)
        for g in range(0, BIG, 8):
            at = pl.ds(base + g, 8)
            total = jnp.sum(part[pl.ds(low + g, 8), :], axis=1, keepdims=True)
            wide_a[at, :] = wide_mu[at, :] / jnp.broadcast_to(total, (8, 128))

    def gathers(r, acc):
        acc = list(acc)
        base = block(r)
        for g in range(0, BIG, 8):
            at = pl.ds(base + g, 8)
            a = wide_a[at, :]
            for c in range(NCH):
                acc[c] = acc[c] + kern[at, pl.ds(c * 128, 128)] * a
            acc[NCH] = acc[NCH] + bin_hot[at, :] * a
        return tuple(acc)

    def sweep(_, carry):
        bin_b, _ = carry
        whole = tree_sum([scale_b[:, pl.ds(c * 128, 128)] for c in range(NCH)])
        whole = jnp.broadcast_to(jnp.sum(whole, axis=1, keepdims=True), (8, 128))
        bin_line = mu_bin / (whole + bin_b)
        sums(0, bin_b, 0)

        @pl.loop(0, steps - 1)
        def _(m):
            sums(2 * m + 1, bin_b, BIG)
            scales(2 * m, 0)
            sums(2 * m + 2, bin_b, 0)
            scales(2 * m + 1, BIG)

        sums(2 * steps - 1, bin_b, BIG)
        scales(2 * steps - 2, 0)
        scales(2 * steps - 1, BIG)
        zero = jnp.zeros((8, 128), jnp.float32)
        acc = lax.fori_loop(0, 2 * steps, gathers, (zero,) * (NCH + 1))
        for c in range(NCH):
            ch = pl.ds(c * 128, 128)
            total = jnp.broadcast_to(jnp.sum(acc[c], axis=0, keepdims=True), (8, 128))
            scale_b[:, ch] = share_b[:, ch] / (total + bin_line)
        bin_acc = jnp.broadcast_to(jnp.sum(acc[NCH], axis=0, keepdims=True), (8, 128))
        bin_sum = jnp.broadcast_to(jnp.sum(bin_acc, axis=1, keepdims=True), (8, 128))
        return nu_bin / (bin_sum + bin_line), bin_line

    ones = jnp.ones((8, 128), jnp.float32)
    bin_b, bin_line = lax.fori_loop(0, ITERS, sweep, (ones, ones))

    @pl.loop(0, (n_rows + BLK - 1) // BLK)
    def _(r):
        spot = pl.ds(pl.multiple_of(r * BLK, BLK), BLK)
        pot = jnp.log(wide_a[spot, :]) - peak[spot, :]
        out[pl.ds(r, 1), :] = jnp.transpose(pot)[:1]

    for c in range(NCH):
        out[NBLK + c : NBLK + c + 1, :] = jnp.log(scale_b[0:1, pl.ds(c * 128, 128)])
    out[32:33, :] = (jnp.log(bin_line) - alpha)[:1]
    out[33:34, :] = jnp.log(bin_b)[:1]


def block_at(params, k, t):
    a = lax.rem(params[0] - k + 4, 4)
    b = lax.rem(params[1] - t + 4, 4)
    return jnp.where(params[2] == 1, a * 4 + b, b * 4 + a)


def pick_kernel(index, counts, pairs, desc, s0, s1, s2, s3, e0, e1, e2, e3, params, sems, more_sems):
    b = index[1]
    copies = []
    for k, target in ((1, s1), (2, s2), (3, s3), (0, s0)):
        p = lax.rem(b + k, 4)
        for side in range(2):
            copy = pltpu.make_async_copy(desc.at[pairs[p, side]], target.at[side], sems.at[k, side])
            copy.start()
            copies.append(copy)
    for k, target in ((1, e1), (2, e2), (3, e3), (0, e0)):
        for m in (1, 2, 3):
            p = lax.rem(b + k - m + 4, 4)
            copy = pltpu.make_async_copy(
                desc.at[pairs[p, 1]], target.at[m - 1], more_sems.at[k, m - 1]
            )
            copy.start()
            copies.append(copy)
    for c in range(4):
        params[c] = index[c]
    for m in range(4):
        p = lax.rem(b - m + 4, 4)
        params[4 + m] = counts[pairs[p, 0]]
        params[8 + m] = counts[pairs[p, 1]]
        params[12 + m] = pairs[p, 0]
        params[16 + m] = p
    for copy in copies:
        copy.wait()


def score_kernel(params, desc, x0, x1, x2, x3, y0, y1, y2, y3, scores, own, others, sems):
    loads = []
    for k, x in enumerate((x0, x1, x2, x3)):
        loads.append(pltpu.make_async_copy(x.at[:, 1], own.at[k], sems.at[0, k]))
    for k, y in enumerate((y0, y1, y2, y3)):
        loads.append(pltpu.make_async_copy(y, others.at[k], sems.at[1, k]))
    for copy in loads:
        copy.start()
    lefts = [desc[params[12 + m]] * jnp.bfloat16(0.0625) for m in range(4)]
    for k in range(4):
        loads[k].wait()
        loads[4 + k].wait()
        for t in range(4):
            spot = pl.ds(pl.multiple_of(block_at(params, k, t) * BLK, BLK), BLK)
            for m in range(4):
                scores[m, :, spot] = lax.dot_general(
                    lefts[m],
                    own[k, t] if m == 0 else others[k, t, m - 1],
                    (((1,), (1,)), ((), ())),
                    preferred_element_type=jnp.float32,
                )


def finish_kernel(params, bins, scores, p0, p1, p2, p3, match, row_bins, col_bins, block, sems):
    alpha = bins[0]
    mine = params[3]
    lanes = lax.broadcasted_iota(jnp.int32, (1, 128), 1)
    row_id = lax.broadcasted_iota(jnp.int32, (BLK, 128), 0)
    quarter = lax.broadcasted_iota(jnp.int32, (4, 128), 0)
    side = jnp.zeros((4, 128), jnp.float32)
    edges = [jnp.zeros((4, 128), jnp.float32)] * NCH
    stores = []
    for m, pay in enumerate((p0, p1, p2, p3)):
        p = params[16 + m]
        n_rows = params[4 + m]
        n_cols = params[8 + m]
        both = n_rows.astype(jnp.float32) + n_cols.astype(jnp.float32)
        norm = -jnp.log(jnp.full((1, 128), both))
        line = pay[pl.ds(mine, 1), :]
        pot = jnp.transpose(jnp.broadcast_to(line, (BLK, 128)))
        row_kept = mine * BLK + row_id < n_rows
        line = jnp.where(mine * BLK + lanes < n_rows, alpha + line + pay[33:34, :] - norm, 0.0)
        side = jnp.where(quarter == p, line, side)
        for c in range(NCH):
            spot = pl.ds(c * 128, 128)
            col_pot = pay[NBLK + c : NBLK + c + 1, :]
            col_kept = c * 128 + lanes < n_cols
            tile = scores[m, :, spot] + pot + col_pot - norm
            block[m, :, spot] = jnp.where(row_kept & col_kept, tile, 0.0)
            line = jnp.where(col_kept, alpha + pay[32:33, :] + col_pot - norm, 0.0)
            edges[c] = jnp.where(quarter == p, line, edges[c])
        copy = pltpu.make_async_copy(block.at[m], match.at[p], sems.at[m])
        copy.start()
        stores.append(copy)
    row_bins[...] = side
    for c in range(NCH):
        col_bins[:, pl.ds(c * 128, 128)] = edges[c]
    for copy in stores:
        copy.wait()


SMEM = functools.partial(pl.BlockSpec, memory_space=pltpu.SMEM)
VMEM = functools.partial(pl.BlockSpec, memory_space=pltpu.VMEM)
ANY = functools.partial(pl.BlockSpec, memory_space=pl.ANY)


def run_sinkhorn(params, bins, xs):
    f32 = jnp.float32
    return pl.pallas_call(
        sinkhorn_kernel,
        out_shape=jax.ShapeDtypeStruct((40, 128), f32),
        in_specs=[SMEM()] * 2 + [ANY()] * 4,
        out_specs=VMEM(),
        scratch_shapes=[
            pltpu.VMEM((KP, KP), f32),
            pltpu.VMEM((BIG, KP), f32),
            pltpu.VMEM((BIG, KP), f32),
            pltpu.VMEM((KP, D), jnp.bfloat16),
            pltpu.VMEM((KP, D), jnp.bfloat16),
            pltpu.VMEM((2 * BIG, 128), f32),
            pltpu.VMEM((KP, 128), f32),
            pltpu.VMEM((KP, 128), f32),
            pltpu.VMEM((KP, 128), f32),
            pltpu.VMEM((KP, 128), f32),
            pltpu.VMEM((8, KP), f32),
            pltpu.VMEM((8, KP), f32),
            pltpu.SemaphoreType.DMA((4, 4, 2)),
        ],
        compiler_params=pltpu.CompilerParams(vmem_limit_bytes=40 * 1024 * 1024),
        cost_estimate=pl.CostEstimate(
            flops=200_000_000_000, bytes_accessed=2 << 20, transcendentals=0
        ),
        name="sinkhorn",
    )(params, bins, *xs)


def run_pick(index, counts, pairs, desc):
    part = jax.ShapeDtypeStruct((2, BLK, D), jnp.bfloat16)
    more = jax.ShapeDtypeStruct((3, BLK, D), jnp.bfloat16)
    return pl.pallas_call(
        pick_kernel,
        out_shape=(part,) * 4 + (more,) * 4 + (jax.ShapeDtypeStruct((20,), jnp.int32),),
        in_specs=[SMEM()] * 3 + [ANY()],
        out_specs=[VMEM()] * 8 + [SMEM()],
        scratch_shapes=[pltpu.SemaphoreType.DMA((4, 2)), pltpu.SemaphoreType.DMA((4, 3))],
        compiler_params=pltpu.CompilerParams(vmem_limit_bytes=6 * 1024 * 1024),
        name="pick",
    )(index, counts, pairs, desc)


def run_scores(params, desc, xs, ys):
    return pl.pallas_call(
        score_kernel,
        out_shape=jax.ShapeDtypeStruct((4, BLK, KP), jnp.float32),
        in_specs=[SMEM(), VMEM()] + [ANY()] * 8,
        out_specs=VMEM(),
        scratch_shapes=[
            pltpu.VMEM((4, 4, BLK, D), jnp.bfloat16),
            pltpu.VMEM((4, 4, 3, BLK, D), jnp.bfloat16),
            pltpu.SemaphoreType.DMA((2, 4)),
        ],
        compiler_params=pltpu.CompilerParams(vmem_limit_bytes=16 * 1024 * 1024),
        cost_estimate=pl.CostEstimate(
            flops=8_000_000_000, bytes_accessed=8 << 20, transcendentals=0
        ),
        name="scores",
    )(params, desc, *xs, *ys)


def run_finish(params, bins, scores, pays):
    f32 = jnp.float32
    return pl.pallas_call(
        finish_kernel,
        out_shape=(
            jax.ShapeDtypeStruct((4, BLK, KP), f32),
            jax.ShapeDtypeStruct((4, BLK), f32),
            jax.ShapeDtypeStruct((4, KP), f32),
        ),
        in_specs=[SMEM()] * 2 + [VMEM()] * 5,
        out_specs=(ANY(), VMEM(), VMEM()),
        scratch_shapes=[pltpu.VMEM((4, BLK, KP), f32), pltpu.SemaphoreType.DMA((4,))],
        compiler_params=pltpu.CompilerParams(vmem_limit_bytes=16 * 1024 * 1024),
        name="finish",
    )(params, bins, scores, *pays)


def shifts(groups, along_b):
    def perm(k):
        moves = []
        for g in range(groups):
            for i in range(4):
                for j in range(4):
                    on_row_1 = (g % 2 == 0) == along_b
                    to = (i, (j + k) % 4) if on_row_1 else ((i + k) % 4, j)
                    moves.append((g * 16 + i * 4 + j, g * 16 + to[0] * 4 + to[1]))
        return moves

    return perm


def on_device(descriptors, counts, pairs, bin_score):
    groups = lax.axis_size("pair")
    even = lax.axis_index("pair") % 2 == 0
    i, j = lax.axis_index("row_0"), lax.axis_index("row_1")
    a, b = jnp.where(even, i, j), jnp.where(even, j, i)
    by_b, by_a = shifts(groups, True), shifts(groups, False)

    index = jnp.stack([a, b, even.astype(jnp.int32), i * 4 + j]).astype(jnp.int32)
    s0, s1, s2, s3, e0, e1, e2, e3, params = run_pick(index, counts, pairs, descriptors)

    def send(parts, moves):
        arrived = []
        for k, x in enumerate(parts, 1):
            arrived.append(lax.ppermute(x, AXES, moves(k)))
        return arrived

    x0 = jnp.stack([s0] + send((s1, s2, s3), by_b))
    xs = [x0] + send((x0, x0, x0), by_a)
    y0 = jnp.stack([e0] + send((e1, e2, e3), by_b))
    ys = [y0] + send((y0, y0, y0), by_a)
    pay = run_sinkhorn(params, bin_score, xs)
    pays = [pay] + [lax.ppermute(pay, AXES, by_b(k)) for k in (1, 2, 3)]
    desc, late = lax.optimization_barrier((descriptors, pay))
    scores = run_scores(params, desc, xs, ys)
    return run_finish(params, bin_score, scores, [late] + pays[1:])


def solution(mesh):
    finer = Mesh(mesh.devices.reshape(mesh.shape["pair"], 4, 4), AXES)
    rows = ("row_0", "row_1")
    in_specs = (P("pair", rows, None), P("pair"), P("pair", None), P())
    out_specs = (P("pair", rows, None), P("pair", rows), P("pair", None))
    return jax.shard_map(
        on_device, mesh=finer, in_specs=in_specs, out_specs=out_specs, check_vma=False
    )
```

profile of v0, /device:TPU:0, one launch (start us, length us, event | category | flops | bytes accessed | tf_op | source)
XLA Modules:
  0.0 90.7 jit_solution(969430164365628116)
XLA Ops:
  0.7 0.8 copy.7.pairs
  1.4 0.1 pad_add_fusion.index
  1.5 1.0 %copy-done = bf16[8,128,256]{2,1,0:T(8,128)(2,1)S(1)} copy-done((bf16[8,128,256]{2,1,0:T(8,128)(2,1)S(1)}, bf16[8,128,256]{2,1,0:T(8,128)(2,1)}, u32[]{:S(2)}) %copy-start) | copy-done | bytes 524312
  2.5 0.7 copy-done.2
  3.2 3.2 %pick.1 = (bf16[2,128,256]{2,1,0:T(8,128)(2,1)S(1)}, bf16[2,128,256]{2,1,0:T(8,128)(2,1)S(1)}, bf16[2,128,256]{2,1,0:T(8,128)(2,1)S(1)}, bf16[2,128,256]{2,1,0:T...) custom-call(s32[4]{0:T(128)S(1)} %pad_add_fusion.index, ...), custom_call_target="tpu_custom_call" | custom-call | tf_op jit(solution)/shard_map/pick/pallas_call | solution.py:323
  6.4 1.8 %collective-permute-start = (bf16[2,128,256]{2,1,0:T(8,128)(2,1)S(1)}, bf16[2,128,256]{2,1,0:T(8,128)(2,1)S(1)}, u32[]{:S(2)}, u32[]{:S(2)}) collective-permute-start(bf16[2,128,256]{2,1,0:T(8,128)(2,1)S(1)} %get-tuple-element.16), channel_id=1, source_target_pairs={{0,1},{1,2},{2,3},{3,0},{4,5},{5,6},{6,7},{7,4},{8,9},{9,10},{10,1... | collective-permute-start | bytes 393224 | tf_op jit(solution)/shard_map/ppermute | solution.py:397
  8.1 2.9 %collective-permute-start.1 = (bf16[2,128,256]{2,1,0:T(8,128)(2,1)S(1)}, bf16[2,128,256]{2,1,0:T(8,128)(2,1)S(1)}, u32[]{:S(2)}, u32[]{:S(2)}) collective-permute-start(bf16[2,128,256]{2,1,0:T(8,128)(2,1)S(1)} %get-tuple-element.17), channel_id=1, source_target_pairs={{0,2},{1,3},{2,0},{3,1},{4,6},{5,7},{6,4},{7,5},{8,10},{9,11},{10,... | collective-permute-start | bytes 393224 | tf_op jit(solution)/shard_map/ppermute | solution.py:397
  11.0 1.3 %collective-permute-start.2 = (bf16[2,128,256]{2,1,0:T(8,128)(2,1)S(1)}, bf16[2,128,256]{2,1,0:T(8,128)(2,1)S(1)}, u32[]{:S(2)}, u32[]{:S(2)}) collective-permute-start(bf16[2,128,256]{2,1,0:T(8,128)(2,1)S(1)} %get-tuple-element.18), channel_id=1, source_target_pairs={{0,3},{1,0},{2,1},{3,2},{4,7},{5,4},{6,5},{7,6},{8,11},{9,8},{10,9... | collective-permute-start | bytes 393224 | tf_op jit(solution)/shard_map/ppermute | solution.py:397
  12.4 0.2 collective-permute-start.7
  12.6 0.0 collective-permute-done
  12.6 2.8 %collective-permute-done.1 = bf16[2,128,256]{2,1,0:T(8,128)(2,1)S(1)} collective-permute-done((bf16[2,128,256]{2,1,0:T(8,128)(2,1)S(1)}, bf16[2,128,256]{2,1,0:T(8,128)(2,1)S(1)}, u32[]{:S(2)}, u32[]{:S(2)}) %collective-permute-start.1) | collective-permute-done | bytes 131104 | tf_op jit(solution)/shard_map/ppermute | solution.py:397
  15.4 0.6 collective-permute-done.2
  16.0 0.1 pad_maximum_fusion.1.x0
  16.1 2.0 %collective-permute-start.3 = (bf16[4,2,128,256]{3,2,1,0:T(8,128)(2,1)S(1)}, bf16[4,2,128,256]{3,2,1,0:T(8,128)(2,1)S(1)}, u32[]{:S(2)}, u32[]{:S(2)}) collective-permute-start(bf16[4,2,128,256]{3,2,1,0:T(8,128)(2,1)S(1)} %pad_maximum_fusion.1.x0), channel_id=1, source_target_pairs={{0,4},{1,5},{2,6},{3,7},{4,8},{5,9},{6,10},{7,11},{8,12},{9,13},{1... | collective-permute-start | bytes 1572872 | tf_op jit(solution)/shard_map/ppermute | solution.py:397
  18.1 3.6 %collective-permute-start.4 = (bf16[4,2,128,256]{3,2,1,0:T(8,128)(2,1)S(1)}, bf16[4,2,128,256]{3,2,1,0:T(8,128)(2,1)S(1)}, u32[]{:S(2)}, u32[]{:S(2)}) collective-permute-start(bf16[4,2,128,256]{3,2,1,0:T(8,128)(2,1)S(1)} %pad_maximum_fusion.1.x0), channel_id=1, source_target_pairs={{0,8},{1,9},{2,10},{3,11},{4,12},{5,13},{6,14},{7,15},{8,0},{9,1},... | collective-permute-start | bytes 1572872 | tf_op jit(solution)/shard_map/ppermute | solution.py:397
  21.7 1.0 %collective-permute-start.5 = (bf16[4,2,128,256]{3,2,1,0:T(8,128)(2,1)S(1)}, bf16[4,2,128,256]{3,2,1,0:T(8,128)(2,1)S(1)}, u32[]{:S(2)}, u32[]{:S(2)}) collective-permute-start(bf16[4,2,128,256]{3,2,1,0:T(8,128)(2,1)S(1)} %pad_maximum_fusion.1.x0), channel_id=1, source_target_pairs={{0,12},{1,13},{2,14},{3,15},{4,0},{5,1},{6,2},{7,3},{8,4},{9,5},{1... | collective-permute-start | bytes 1572872 | tf_op jit(solution)/shard_map/ppermute | solution.py:397
  22.7 2.6 %collective-permute-start.8 = (bf16[3,128,256]{2,1,0:T(8,128)(2,1)S(1)}, bf16[3,128,256]{2,1,0:T(8,128)(2,1)S(1)}, u32[]{:S(2)}, u32[]{:S(2)}) collective-permute-start(bf16[3,128,256]{2,1,0:T(8,128)(2,1)S(1)} %get-tuple-element.23), channel_id=1, source_target_pairs={{0,3},{1,0},{2,1},{3,2},{4,7},{5,4},{6,5},{7,6},{8,11},{9,8},{10,9... | collective-permute-start | bytes 589832 | tf_op jit(solution)/shard_map/ppermute | solution.py:397
  25.9 4.6 %collective-permute-done.8 = bf16[3,128,256]{2,1,0:T(8,128)(2,1)S(1)} collective-permute-done((bf16[3,128,256]{2,1,0:T(8,128)(2,1)S(1)}, bf16[3,128,256]{2,1,0:T(8,128)(2,1)S(1)}, u32[]{:S(2)}, u32[]{:S(2)}) %collective-permute-start.8) | collective-permute-done | bytes 196640 | tf_op jit(solution)/shard_map/ppermute | solution.py:397
  30.5 4.2 %collective-permute-done.6 = bf16[3,128,256]{2,1,0:T(8,128)(2,1)S(1)} collective-permute-done((bf16[3,128,256]{2,1,0:T(8,128)(2,1)S(1)}, bf16[3,128,256]{2,1,0:T(8,128)(2,1)S(1)}, u32[]{:S(2)}, u32[]{:S(2)}) %collective-permute-start.6) | collective-permute-done | bytes 196640 | tf_op jit(solution)/shard_map/ppermute | solution.py:397
  34.8 1.0 %pad_maximum_fusion.y0 = bf16[4,3,128,256]{3,2,1,0:T(8,128)(2,1)} fusion(bf16[1,3,128,256]{3,2,1,0:T(8,128)(2,1)S(1)} %bitcast.15, bf16[1,3,128,256]{3,2,1,0:T(8,128)(2,1)S(1)} %bitcast.14, bf16[1,3,128,256]{3,2,1,0:T(8,128)(2,1)S(1)} %bitcast.16, bf16[1,3,128,256]{3,2,1,0:T(8,128)(2,1)S(1)} %bitcast.12), kind=kLoop, calls=%fused_computation | loop fusion | flops 1179648 | bytes 1572864 | tf_op jit(solution)/shard_map/stack | solution.py:402
  35.7 2.8 %collective-permute-start.10 = (bf16[4,3,128,256]{3,2,1,0:T(8,128)(2,1)}, bf16[4,3,128,256]{3,2,1,0:T(8,128)(2,1)}, u32[]{:S(2)}, u32[]{:S(2)}) collective-permute-start(bf16[4,3,128,256]{3,2,1,0:T(8,128)(2,1)} %pad_maximum_fusion.y0), channel_id=1, source_target_pairs={{0,8},{1,9},{2,10},{3,11},{4,12},{5,13},{6,14},{7,15},{8,0},{9,1},... | collective-permute-start | bytes 2359304 | tf_op jit(solution)/shard_map/ppermute | solution.py:397
  38.5 1.0 %collective-permute-start.11 = (bf16[4,3,128,256]{3,2,1,0:T(8,128)(2,1)}, bf16[4,3,128,256]{3,2,1,0:T(8,128)(2,1)}, u32[]{:S(2)}, u32[]{:S(2)}) collective-permute-start(bf16[4,3,128,256]{3,2,1,0:T(8,128)(2,1)} %pad_maximum_fusion.y0), channel_id=1, source_target_pairs={{0,12},{1,13},{2,14},{3,15},{4,0},{5,1},{6,2},{7,3},{8,4},{9,5},{1... | collective-permute-start | bytes 2359304 | tf_op jit(solution)/shard_map/ppermute | solution.py:397
  39.6 0.0 collective-permute-done.3.x1
  39.6 1.0 %collective-permute-start.9 = (bf16[4,3,128,256]{3,2,1,0:T(8,128)(2,1)}, bf16[4,3,128,256]{3,2,1,0:T(8,128)(2,1)}, u32[]{:S(2)}, u32[]{:S(2)}) collective-permute-start(bf16[4,3,128,256]{3,2,1,0:T(8,128)(2,1)} %pad_maximum_fusion.y0), channel_id=1, source_target_pairs={{0,4},{1,5},{2,6},{3,7},{4,8},{5,9},{6,10},{7,11},{8,12},{9,13},{1... | collective-permute-start | bytes 2359304 | tf_op jit(solution)/shard_map/ppermute | solution.py:397
  40.6 0.0 collective-permute-done.4.x2
  40.6 0.0 collective-permute-done.5.x3
  40.6 39.3 %sinkhorn.1.p0 = f32[40,128]{1,0:T(8,128)S(1)} custom-call(s32[20]{0:T(128)S(1)} %get-tuple-element.14.params, f32[1]{0:T(128)S(6)} %copy.8.bins, bf16[4,2,128,256]{3,2,1,0:T(8,128)(2,1)S(1)} %pad_maximum_fusion.1.x0, bf16[4,2,128,256]{3,2,1,0:T(8,128)(2,1)S(1)} %collective-permute-done.3.x1, bf16[4,2,128,256]{3,2,1,0:T(8,128)(2,1)S(1)} %collective-permute-done.4.x2, ...), custom_call_target="tpu_custom_call" | custom-call | flops 199999995904 | bytes 2097152 | tf_op jit(solution)/shard_map/sinkhorn/pallas_call | solution.py:292
  79.9 0.1 collective-permute-start.12
  80.0 1.2 %collective-permute-start.13 = (f32[40,128]{1,0:T(8,128)S(1)}, f32[40,128]{1,0:T(8,128)S(1)}, u32[]{:S(2)}, u32[]{:S(2)}) collective-permute-start(f32[40,128]{1,0:T(8,128)S(1)} %sinkhorn.1.p0), channel_id=1, source_target_pairs={{0,2},{1,3},{2,0},{3,1},{4,6},{5,7},{6,4},{7,5},{8,10},{9,11},{10,... | collective-permute-start | bytes 61448 | tf_op jit(solution)/shard_map/ppermute | solution.py:405
  81.2 2.0 %collective-permute-start.14 = (f32[40,128]{1,0:T(8,128)S(1)}, f32[40,128]{1,0:T(8,128)S(1)}, u32[]{:S(2)}, u32[]{:S(2)}) collective-permute-start(f32[40,128]{1,0:T(8,128)S(1)} %sinkhorn.1.p0), channel_id=1, source_target_pairs={{0,3},{1,0},{2,1},{3,2},{4,7},{5,4},{6,5},{7,6},{8,11},{9,8},{10,9... | collective-permute-start | bytes 61448 | tf_op jit(solution)/shard_map/ppermute | solution.py:405
  83.3 3.6 %scores.1 = f32[4,128,2048]{2,1,0:T(8,128)S(1)} custom-call(s32[20]{0:T(128)S(1)} %get-tuple-element.14.params, bf16[8,128,256]{2,1,0:T(8,128)(2,1)S(1)} %copy-done.1, bf16[4,2,128,256]{3,2,1,0:T(8,128)(2,1)S(1)} %pad_maximum_fusion.1.x0, bf16[4,2,128,256]{3,2,1,0:T(8,128)(2,1)S(1)} %collective-permute-done.3.x1, ...), custom_call_target="tpu_custom_call" | custom-call | flops 8000000000 | bytes 8388608 | tf_op jit(solution)/shard_map/scores/pallas_call | solution.py:335
  86.9 3.7 %finish.1 = (f32[4,128,2048]{2,1,0:T(8,128)}, f32[4,128]{1,0:T(4,128)}, f32[4,2048]{1,0:T(4,128)}) custom-call(s32[20]{0:T(128)S(1)} %get-tuple-element.14.params, f32[1]{0:T(128)S(6)} %copy.8.bins, f32[4,128,2048]{2,1,0:T(8,128)S(1)} %scores.1, f32[40,128]{1,0:T(8,128)S(1)} %sinkhorn.1.p0, f32[40,128]{1,0:T(8,128)S(1)} %collective-permute-done.12.p1, ...), custom_call_target="tpu_custom_call" | custom-call | tf_op jit(solution)/shard_map/finish/pallas_call | solution.py:355
  (12 shorter events, 0.0 us)
Async XLA Ops:
  1.5 1.0 %copy-start = (bf16[8,128,256]{2,1,0:T(8,128)(2,1)S(1)}, bf16[8,128,256]{2,1,0:T(8,128)(2,1)}, u32[]{:S(2)}) copy-start(bf16[8,128,256]{2,1,0:T(8,128)(2,1)} %desc.2) | copy-start | bytes 1572868
  2.5 0.7 copy-start.2
  6.4 6.2 %collective-permute-start = (bf16[2,128,256]{2,1,0:T(8,128)(2,1)S(1)}, bf16[2,128,256]{2,1,0:T(8,128)(2,1)S(1)}, u32[]{:S(2)}, u32[]{:S(2)}) collective-permute-start(bf16[2,128,256]{2,1,0:T(8,128)(2,1)S(1)} %get-tuple-element.16), channel_id=1, source_target_pairs={{0,1},{1,2},{2,3},{3,0},{4,5},{5,6},{6,7},{7,4},{8,9},{9,10},{10,1... | collective-permute-start | bytes 393224 | tf_op jit(solution)/shard_map/ppermute | solution.py:397
  8.1 7.2 %collective-permute-start.1 = (bf16[2,128,256]{2,1,0:T(8,128)(2,1)S(1)}, bf16[2,128,256]{2,1,0:T(8,128)(2,1)S(1)}, u32[]{:S(2)}, u32[]{:S(2)}) collective-permute-start(bf16[2,128,256]{2,1,0:T(8,128)(2,1)S(1)} %get-tuple-element.17), channel_id=1, source_target_pairs={{0,2},{1,3},{2,0},{3,1},{4,6},{5,7},{6,4},{7,5},{8,10},{9,11},{10,... | collective-permute-start | bytes 393224 | tf_op jit(solution)/shard_map/ppermute | solution.py:397
  11.0 5.0 %collective-permute-start.2 = (bf16[2,128,256]{2,1,0:T(8,128)(2,1)S(1)}, bf16[2,128,256]{2,1,0:T(8,128)(2,1)S(1)}, u32[]{:S(2)}, u32[]{:S(2)}) collective-permute-start(bf16[2,128,256]{2,1,0:T(8,128)(2,1)S(1)} %get-tuple-element.18), channel_id=1, source_target_pairs={{0,3},{1,0},{2,1},{3,2},{4,7},{5,4},{6,5},{7,6},{8,11},{9,8},{10,9... | collective-permute-start | bytes 393224 | tf_op jit(solution)/shard_map/ppermute | solution.py:397
  12.4 12.8 %collective-permute-start.7 = (bf16[3,128,256]{2,1,0:T(8,128)(2,1)S(1)}, bf16[3,128,256]{2,1,0:T(8,128)(2,1)S(1)}, u32[]{:S(2)}, u32[]{:S(2)}) collective-permute-start(bf16[3,128,256]{2,1,0:T(8,128)(2,1)S(1)} %get-tuple-element.22), channel_id=1, source_target_pairs={{0,2},{1,3},{2,0},{3,1},{4,6},{5,7},{6,4},{7,5},{8,10},{9,11},{10,... | collective-permute-start | bytes 589832 | tf_op jit(solution)/shard_map/ppermute | solution.py:397
  16.1 23.5 %collective-permute-start.3 = (bf16[4,2,128,256]{3,2,1,0:T(8,128)(2,1)S(1)}, bf16[4,2,128,256]{3,2,1,0:T(8,128)(2,1)S(1)}, u32[]{:S(2)}, u32[]{:S(2)}) collective-permute-start(bf16[4,2,128,256]{3,2,1,0:T(8,128)(2,1)S(1)} %pad_maximum_fusion.1.x0), channel_id=1, source_target_pairs={{0,4},{1,5},{2,6},{3,7},{4,8},{5,9},{6,10},{7,11},{8,12},{9,13},{1... | collective-permute-start | bytes 1572872 | tf_op jit(solution)/shard_map/ppermute | solution.py:397
  18.1 22.5 %collective-permute-start.4 = (bf16[4,2,128,256]{3,2,1,0:T(8,128)(2,1)S(1)}, bf16[4,2,128,256]{3,2,1,0:T(8,128)(2,1)S(1)}, u32[]{:S(2)}, u32[]{:S(2)}) collective-permute-start(bf16[4,2,128,256]{3,2,1,0:T(8,128)(2,1)S(1)} %pad_maximum_fusion.1.x0), channel_id=1, source_target_pairs={{0,8},{1,9},{2,10},{3,11},{4,12},{5,13},{6,14},{7,15},{8,0},{9,1},... | collective-permute-start | bytes 1572872 | tf_op jit(solution)/shard_map/ppermute | solution.py:397
  21.7 18.9 %collective-permute-start.5 = (bf16[4,2,128,256]{3,2,1,0:T(8,128)(2,1)S(1)}, bf16[4,2,128,256]{3,2,1,0:T(8,128)(2,1)S(1)}, u32[]{:S(2)}, u32[]{:S(2)}) collective-permute-start(bf16[4,2,128,256]{3,2,1,0:T(8,128)(2,1)S(1)} %pad_maximum_fusion.1.x0), channel_id=1, source_target_pairs={{0,12},{1,13},{2,14},{3,15},{4,0},{5,1},{6,2},{7,3},{8,4},{9,5},{1... | collective-permute-start | bytes 1572872 | tf_op jit(solution)/shard_map/ppermute | solution.py:397
  22.7 7.9 %collective-permute-start.8 = (bf16[3,128,256]{2,1,0:T(8,128)(2,1)S(1)}, bf16[3,128,256]{2,1,0:T(8,128)(2,1)S(1)}, u32[]{:S(2)}, u32[]{:S(2)}) collective-permute-start(bf16[3,128,256]{2,1,0:T(8,128)(2,1)S(1)} %get-tuple-element.23), channel_id=1, source_target_pairs={{0,3},{1,0},{2,1},{3,2},{4,7},{5,4},{6,5},{7,6},{8,11},{9,8},{10,9... | collective-permute-start | bytes 589832 | tf_op jit(solution)/shard_map/ppermute | solution.py:397
  25.2 9.5 %collective-permute-start.6 = (bf16[3,128,256]{2,1,0:T(8,128)(2,1)S(1)}, bf16[3,128,256]{2,1,0:T(8,128)(2,1)S(1)}, u32[]{:S(2)}, u32[]{:S(2)}) collective-permute-start(bf16[3,128,256]{2,1,0:T(8,128)(2,1)S(1)} %get-tuple-element.21), channel_id=1, source_target_pairs={{0,1},{1,2},{2,3},{3,0},{4,5},{5,6},{6,7},{7,4},{8,9},{9,10},{10,1... | collective-permute-start | bytes 589832 | tf_op jit(solution)/shard_map/ppermute | solution.py:397
  35.7 45.5 %collective-permute-start.10 = (bf16[4,3,128,256]{3,2,1,0:T(8,128)(2,1)}, bf16[4,3,128,256]{3,2,1,0:T(8,128)(2,1)}, u32[]{:S(2)}, u32[]{:S(2)}) collective-permute-start(bf16[4,3,128,256]{3,2,1,0:T(8,128)(2,1)} %pad_maximum_fusion.y0), channel_id=1, source_target_pairs={{0,8},{1,9},{2,10},{3,11},{4,12},{5,13},{6,14},{7,15},{8,0},{9,1},... | collective-permute-start | bytes 2359304 | tf_op jit(solution)/shard_map/ppermute | solution.py:397
  38.5 44.7 %collective-permute-start.11 = (bf16[4,3,128,256]{3,2,1,0:T(8,128)(2,1)}, bf16[4,3,128,256]{3,2,1,0:T(8,128)(2,1)}, u32[]{:S(2)}, u32[]{:S(2)}) collective-permute-start(bf16[4,3,128,256]{3,2,1,0:T(8,128)(2,1)} %pad_maximum_fusion.y0), channel_id=1, source_target_pairs={{0,12},{1,13},{2,14},{3,15},{4,0},{5,1},{6,2},{7,3},{8,4},{9,5},{1... | collective-permute-start | bytes 2359304 | tf_op jit(solution)/shard_map/ppermute | solution.py:397
  39.6 43.7 %collective-permute-start.9 = (bf16[4,3,128,256]{3,2,1,0:T(8,128)(2,1)}, bf16[4,3,128,256]{3,2,1,0:T(8,128)(2,1)}, u32[]{:S(2)}, u32[]{:S(2)}) collective-permute-start(bf16[4,3,128,256]{3,2,1,0:T(8,128)(2,1)} %pad_maximum_fusion.y0), channel_id=1, source_target_pairs={{0,4},{1,5},{2,6},{3,7},{4,8},{5,9},{6,10},{7,11},{8,12},{9,13},{1... | collective-permute-start | bytes 2359304 | tf_op jit(solution)/shard_map/ppermute | solution.py:397
  40.6 42.7 %copy-start.1 = (bf16[8,128,256]{2,1,0:T(8,128)(2,1)S(1)}, bf16[8,128,256]{2,1,0:T(8,128)(2,1)}, u32[]{:S(2)}) copy-start(bf16[8,128,256]{2,1,0:T(8,128)(2,1)} %desc.2) | copy-start | bytes 1572868
  79.9 6.9 %collective-permute-start.12 = (f32[40,128]{1,0:T(8,128)S(1)}, f32[40,128]{1,0:T(8,128)S(1)}, u32[]{:S(2)}, u32[]{:S(2)}) collective-permute-start(f32[40,128]{1,0:T(8,128)S(1)} %sinkhorn.1.p0), channel_id=1, source_target_pairs={{0,1},{1,2},{2,3},{3,0},{4,5},{5,6},{6,7},{7,4},{8,9},{9,10},{10,1... | collective-permute-start | bytes 61448 | tf_op jit(solution)/shard_map/ppermute | solution.py:405
  80.0 6.8 %collective-permute-start.13 = (f32[40,128]{1,0:T(8,128)S(1)}, f32[40,128]{1,0:T(8,128)S(1)}, u32[]{:S(2)}, u32[]{:S(2)}) collective-permute-start(f32[40,128]{1,0:T(8,128)S(1)} %sinkhorn.1.p0), channel_id=1, source_target_pairs={{0,2},{1,3},{2,0},{3,1},{4,6},{5,7},{6,4},{7,5},{8,10},{9,11},{10,... | collective-permute-start | bytes 61448 | tf_op jit(solution)/shard_map/ppermute | solution.py:405
  81.2 5.7 %collective-permute-start.14 = (f32[40,128]{1,0:T(8,128)S(1)}, f32[40,128]{1,0:T(8,128)S(1)}, u32[]{:S(2)}, u32[]{:S(2)}) collective-permute-start(f32[40,128]{1,0:T(8,128)S(1)} %sinkhorn.1.p0), channel_id=1, source_target_pairs={{0,3},{1,0},{2,1},{3,2},{4,7},{5,4},{6,5},{7,6},{8,11},{9,8},{10,9... | collective-permute-start | bytes 61448 | tf_op jit(solution)/shard_map/ppermute | solution.py:405
where the time goes:
time: 90.9 us; the launch traced here: 90.7 us
  Pallas kernels  49.8 us (55%)
  starting transfers between devices  23.5 us (26%)
  waiting for transfers between devices  12.3 us (14%)
  local copies, waits for them, and re-layouts  2.47 us (3%)
  between operations  1.55 us (2%)
  other arithmetic  1.12 us (1%)
    pallas_call x1, Pallas kernels, run_sinkhorn(): pl.pallas_call(sinkhorn_kernel, out_shape=jax.ShapeDtypeStruct((40, 128),...  39.3 us
    ppermute x12, starting transfers between devices, send(): arrived.append(lax.ppermute(x, AXES, moves(k)))  20.2 us
    ppermute x12, waiting for transfers between devices, send(): arrived.append(lax.ppermute(x, AXES, moves(k)))  12.3 us
    pallas_call x1, Pallas kernels, run_finish(): pl.pallas_call(finish_kernel, out_shape=(jax.ShapeDtypeStruct((4, BLK, KP...  3.66 us
    pallas_call x1, Pallas kernels, run_scores(): pl.pallas_call(score_kernel, out_shape=jax.ShapeDtypeStruct((4, BLK, KP),...  3.58 us
    ppermute x3, starting transfers between devices, on_device(): pays = [pay] + [lax.ppermute(pay, AXES, by_b(k)) for k in (1, 2, 3)]  3.3 us
    pallas_call x1, Pallas kernels, run_pick(): pl.pallas_call(pick_kernel, out_shape=(part,) * 4 + (more,) * 4 + (jax.Sh...  3.19 us
    unnamed x7, local copies, waits for them, and re-layouts  2.47 us
  transfers between devices with their start and end apart: 15, of which 4 were waited for; matrix products, arithmetic and copies ran while one was open for 1% of the time, Pallas kernels for 47%

commit v1 on v0

--- a/solution.py
+++ b/solution.py
@@ -56,19 +56,23 @@
     out[...] = jnp.zeros_like(out)
     pair_rows = 2 * BIG
     steps = (n_rows + pair_rows - 1) // pair_rows
+
+    @pl.loop(0, NBLK)
+    def _(c):
+        for g in range(0, BLK, 8):
+            at = pl.ds(pl.multiple_of(c * BLK + g, 8), 8)
+            row = c * BLK + g + lax.broadcasted_iota(jnp.int32, (8, 128), 0)
+            wide_mu[at, :] = jnp.where(row < n_rows, mu, 0.0)
+
     for copy in copies:
         copy.wait()
 
-    @pl.loop(0, NBLK)
+    @pl.loop(n_cols // BLK, NBLK)
     def _(c):
         spot = pl.ds(pl.multiple_of(c * BLK, BLK), BLK)
         place = c * BLK + lax.broadcasted_iota(jnp.int32, (BLK, D), 0)
         kept = jnp.where(place < n_cols, 1.0, 0.0)
         cols[spot, :] = (cols[spot, :].astype(jnp.float32) * kept).astype(jnp.bfloat16)
-        for g in range(0, BLK, 8):
-            at = pl.ds(pl.multiple_of(c * BLK + g, 8), 8)
-            row = c * BLK + g + lax.broadcasted_iota(jnp.int32, (8, 128), 0)
-            wide_mu[at, :] = jnp.where(row < n_rows, mu, 0.0)
 
     def block(r):
         return pl.multiple_of(r * BIG, BIG)
@@ -101,16 +105,25 @@
             bin_hot[at, :] = jnp.where(lanes == 0, jnp.exp(alpha - drop), 0.0)
 
     scores_of(0, raw_0)
+    once = jnp.minimum(n_cols, 1)
 
     @pl.loop(0, steps - 1)
     def _(m):
-        scores_of(2 * m + 1, raw_1)
-        exps_of(2 * m, raw_0)
-        scores_of(2 * m + 2, raw_0)
-        exps_of(2 * m + 1, raw_1)
-
-    scores_of(2 * steps - 1, raw_1)
-    exps_of(2 * steps - 2, raw_0)
+        @pl.loop(0, once)
+        def _(_):
+            scores_of(2 * m + 1, raw_1)
+            exps_of(2 * m, raw_0)
+
+        @pl.loop(0, once)
+        def _(_):
+            scores_of(2 * m + 2, raw_0)
+            exps_of(2 * m + 1, raw_1)
+
+    @pl.loop(0, once)
+    def _(_):
+        scores_of(2 * steps - 1, raw_1)
+        exps_of(2 * steps - 2, raw_0)
+
     exps_of(2 * steps - 1, raw_1)
 
     def sums(r, bin_b, low):
@@ -192,20 +205,24 @@
     return jnp.where(params[2] == 1, a * 4 + b, b * 4 + a)
 
 
-def pick_kernel(index, counts, pairs, desc, s0, s1, s2, s3, e0, e1, e2, e3, params, sems, more_sems):
+def pick_kernel(index, desc, s0, s1, s2, s3, e0, e1, e2, e3, params, sems, more_sems):
     b = index[1]
+
+    def image(p, side):
+        return index[12 + 2 * p + side]
+
     copies = []
     for k, target in ((1, s1), (2, s2), (3, s3), (0, s0)):
         p = lax.rem(b + k, 4)
         for side in range(2):
-            copy = pltpu.make_async_copy(desc.at[pairs[p, side]], target.at[side], sems.at[k, side])
+            copy = pltpu.make_async_copy(desc.at[image(p, side)], target.at[side], sems.at[k, side])
             copy.start()
             copies.append(copy)
     for k, target in ((1, e1), (2, e2), (3, e3), (0, e0)):
         for m in (1, 2, 3):
             p = lax.rem(b + k - m + 4, 4)
             copy = pltpu.make_async_copy(
-                desc.at[pairs[p, 1]], target.at[m - 1], more_sems.at[k, m - 1]
+                desc.at[image(p, 1)], target.at[m - 1], more_sems.at[k, m - 1]
             )
             copy.start()
             copies.append(copy)
@@ -213,9 +230,9 @@
         params[c] = index[c]
     for m in range(4):
         p = lax.rem(b - m + 4, 4)
-        params[4 + m] = counts[pairs[p, 0]]
-        params[8 + m] = counts[pairs[p, 1]]
-        params[12 + m] = pairs[p, 0]
+        params[4 + m] = index[4 + image(p, 0)]
+        params[8 + m] = index[4 + image(p, 1)]
+        params[12 + m] = image(p, 0)
         params[16 + m] = p
     for copy in copies:
         copy.wait()
@@ -317,18 +334,18 @@
     )(params, bins, *xs)
 
 
-def run_pick(index, counts, pairs, desc):
+def run_pick(index, desc):
     part = jax.ShapeDtypeStruct((2, BLK, D), jnp.bfloat16)
     more = jax.ShapeDtypeStruct((3, BLK, D), jnp.bfloat16)
     return pl.pallas_call(
         pick_kernel,
         out_shape=(part,) * 4 + (more,) * 4 + (jax.ShapeDtypeStruct((20,), jnp.int32),),
-        in_specs=[SMEM()] * 3 + [ANY()],
+        in_specs=[SMEM(), ANY()],
         out_specs=[VMEM()] * 8 + [SMEM()],
         scratch_shapes=[pltpu.SemaphoreType.DMA((4, 2)), pltpu.SemaphoreType.DMA((4, 3))],
         compiler_params=pltpu.CompilerParams(vmem_limit_bytes=6 * 1024 * 1024),
         name="pick",
-    )(index, counts, pairs, desc)
+    )(index, desc)
 
 
 def run_scores(params, desc, xs, ys):
@@ -389,7 +406,8 @@
     by_b, by_a = shifts(groups, True), shifts(groups, False)
 
     index = jnp.stack([a, b, even.astype(jnp.int32), i * 4 + j]).astype(jnp.int32)
-    s0, s1, s2, s3, e0, e1, e2, e3, params = run_pick(index, counts, pairs, descriptors)
+    index = jnp.concatenate([index, counts, pairs.reshape(-1)])
+    s0, s1, s2, s3, e0, e1, e2, e3, params = run_pick(index, descriptors)
 
     def send(parts, moves):
         arrived = []

time: 90.9 us -> 90.3 us (level)
    unnamed x7 -> x5, local copies, waits for them, and re-layouts: 2.47 us -> 1.81 us
where the time goes in v1:
time: 90.3 us; the launch traced here: 90.1 us
  Pallas kernels  49.1 us (54%)
  starting transfers between devices  23.5 us (26%)
  waiting for transfers between devices  12.3 us (14%)
  local copies, waits for them, and re-layouts  2.63 us (3%)
  between operations  1.55 us (2%)
  other arithmetic  1.05 us (1%)
    pallas_call x1, Pallas kernels, run_sinkhorn(): pl.pallas_call(sinkhorn_kernel, out_shape=jax.ShapeDtypeStruct((40, 128),...  38.7 us
    ppermute x12, starting transfers between devices, send(): arrived.append(lax.ppermute(x, AXES, moves(k)))  20.2 us
    ppermute x12, waiting for transfers between devices, send(): arrived.append(lax.ppermute(x, AXES, moves(k)))  12.3 us
    pallas_call x1, Pallas kernels, run_finish(): pl.pallas_call(finish_kernel, out_shape=(jax.ShapeDtypeStruct((4, BLK, KP...  3.66 us
    pallas_call x1, Pallas kernels, run_scores(): pl.pallas_call(score_kernel, out_shape=jax.ShapeDtypeStruct((4, BLK, KP),...  3.58 us
    ppermute x3, starting transfers between devices, on_device(): pays = [pay] + [lax.ppermute(pay, AXES, by_b(k)) for k in (1, 2, 3)]  3.3 us
    pallas_call x1, Pallas kernels, run_pick(): pl.pallas_call(pick_kernel, out_shape=(part,) * 4 + (more,) * 4 + (jax.Sh...  3.15 us
    unnamed x5, local copies, waits for them, and re-layouts  1.81 us
  transfers between devices with their start and end apart: 15, of which 4 were waited for; matrix products, arithmetic and copies ran while one was open for 1% of the time, Pallas kernels for 47%

profile of v1, /device:TPU:0, one launch (start us, length us, event | category | flops | bytes accessed | tf_op | source)
XLA Modules:
  0.0 90.1 jit_solution(18208209362187381692)
XLA Ops:
  0.7 0.8 copy.8
  1.4 0.1 reshape.9
  1.5 0.7 concatenate.3.index
  2.2 1.0 %copy-done = bf16[8,128,256]{2,1,0:T(8,128)(2,1)S(1)} copy-done((bf16[8,128,256]{2,1,0:T(8,128)(2,1)S(1)}, bf16[8,128,256]{2,1,0:T(8,128)(2,1)}, u32[]{:S(2)}) %copy-start) | copy-done | bytes 524312
  3.3 3.2 %pick.1 = (bf16[2,128,256]{2,1,0:T(8,128)(2,1)S(1)}, bf16[2,128,256]{2,1,0:T(8,128)(2,1)S(1)}, bf16[2,128,256]{2,1,0:T(8,128)(2,1)S(1)}, bf16[2,128,256]{2,1,0:T...) custom-call(s32[20]{0:T(128)S(1)} %concatenate.3.index, ...), custom_call_target="tpu_custom_call" | custom-call | tf_op jit(solution)/shard_map/pick/pallas_call | solution.py:340
  6.4 1.8 %collective-permute-start = (bf16[2,128,256]{2,1,0:T(8,128)(2,1)S(1)}, bf16[2,128,256]{2,1,0:T(8,128)(2,1)S(1)}, u32[]{:S(2)}, u32[]{:S(2)}) collective-permute-start(bf16[2,128,256]{2,1,0:T(8,128)(2,1)S(1)} %get-tuple-element.16), channel_id=1, source_target_pairs={{0,1},{1,2},{2,3},{3,0},{4,5},{5,6},{6,7},{7,4},{8,9},{9,10},{10,1... | collective-permute-start | bytes 393224 | tf_op jit(solution)/shard_map/ppermute | solution.py:415
  8.2 2.9 %collective-permute-start.1 = (bf16[2,128,256]{2,1,0:T(8,128)(2,1)S(1)}, bf16[2,128,256]{2,1,0:T(8,128)(2,1)S(1)}, u32[]{:S(2)}, u32[]{:S(2)}) collective-permute-start(bf16[2,128,256]{2,1,0:T(8,128)(2,1)S(1)} %get-tuple-element.17), channel_id=1, source_target_pairs={{0,2},{1,3},{2,0},{3,1},{4,6},{5,7},{6,4},{7,5},{8,10},{9,11},{10,... | collective-permute-start | bytes 393224 | tf_op jit(solution)/shard_map/ppermute | solution.py:415
  11.1 1.3 %collective-permute-start.2 = (bf16[2,128,256]{2,1,0:T(8,128)(2,1)S(1)}, bf16[2,128,256]{2,1,0:T(8,128)(2,1)S(1)}, u32[]{:S(2)}, u32[]{:S(2)}) collective-permute-start(bf16[2,128,256]{2,1,0:T(8,128)(2,1)S(1)} %get-tuple-element.18), channel_id=1, source_target_pairs={{0,3},{1,0},{2,1},{3,2},{4,7},{5,4},{6,5},{7,6},{8,11},{9,8},{10,9... | collective-permute-start | bytes 393224 | tf_op jit(solution)/shard_map/ppermute | solution.py:415
  12.5 0.2 collective-permute-start.7
  12.7 0.0 collective-permute-done
  12.7 2.8 %collective-permute-done.1 = bf16[2,128,256]{2,1,0:T(8,128)(2,1)S(1)} collective-permute-done((bf16[2,128,256]{2,1,0:T(8,128)(2,1)S(1)}, bf16[2,128,256]{2,1,0:T(8,128)(2,1)S(1)}, u32[]{:S(2)}, u32[]{:S(2)}) %collective-permute-start.1) | collective-permute-done | bytes 131104 | tf_op jit(solution)/shard_map/ppermute | solution.py:415
  15.4 0.6 collective-permute-done.2
  16.1 0.1 pad_maximum_fusion.1.x0
  16.1 2.0 %collective-permute-start.3 = (bf16[4,2,128,256]{3,2,1,0:T(8,128)(2,1)S(1)}, bf16[4,2,128,256]{3,2,1,0:T(8,128)(2,1)S(1)}, u32[]{:S(2)}, u32[]{:S(2)}) collective-permute-start(bf16[4,2,128,256]{3,2,1,0:T(8,128)(2,1)S(1)} %pad_maximum_fusion.1.x0), channel_id=1, source_target_pairs={{0,4},{1,5},{2,6},{3,7},{4,8},{5,9},{6,10},{7,11},{8,12},{9,13},{1... | collective-permute-start | bytes 1572872 | tf_op jit(solution)/shard_map/ppermute | solution.py:415
  18.1 3.6 %collective-permute-start.4 = (bf16[4,2,128,256]{3,2,1,0:T(8,128)(2,1)S(1)}, bf16[4,2,128,256]{3,2,1,0:T(8,128)(2,1)S(1)}, u32[]{:S(2)}, u32[]{:S(2)}) collective-permute-start(bf16[4,2,128,256]{3,2,1,0:T(8,128)(2,1)S(1)} %pad_maximum_fusion.1.x0), channel_id=1, source_target_pairs={{0,8},{1,9},{2,10},{3,11},{4,12},{5,13},{6,14},{7,15},{8,0},{9,1},... | collective-permute-start | bytes 1572872 | tf_op jit(solution)/shard_map/ppermute | solution.py:415
  21.7 1.0 %collective-permute-start.5 = (bf16[4,2,128,256]{3,2,1,0:T(8,128)(2,1)S(1)}, bf16[4,2,128,256]{3,2,1,0:T(8,128)(2,1)S(1)}, u32[]{:S(2)}, u32[]{:S(2)}) collective-permute-start(bf16[4,2,128,256]{3,2,1,0:T(8,128)(2,1)S(1)} %pad_maximum_fusion.1.x0), channel_id=1, source_target_pairs={{0,12},{1,13},{2,14},{3,15},{4,0},{5,1},{6,2},{7,3},{8,4},{9,5},{1... | collective-permute-start | bytes 1572872 | tf_op jit(solution)/shard_map/ppermute | solution.py:415
  22.7 2.6 %collective-permute-start.8 = (bf16[3,128,256]{2,1,0:T(8,128)(2,1)S(1)}, bf16[3,128,256]{2,1,0:T(8,128)(2,1)S(1)}, u32[]{:S(2)}, u32[]{:S(2)}) collective-permute-start(bf16[3,128,256]{2,1,0:T(8,128)(2,1)S(1)} %get-tuple-element.23), channel_id=1, source_target_pairs={{0,3},{1,0},{2,1},{3,2},{4,7},{5,4},{6,5},{7,6},{8,11},{9,8},{10,9... | collective-permute-start | bytes 589832 | tf_op jit(solution)/shard_map/ppermute | solution.py:415
  25.3 0.0 collective-permute-done.7
  25.3 0.0 collective-permute-start.6
  25.9 4.6 %collective-permute-done.8 = bf16[3,128,256]{2,1,0:T(8,128)(2,1)S(1)} collective-permute-done((bf16[3,128,256]{2,1,0:T(8,128)(2,1)S(1)}, bf16[3,128,256]{2,1,0:T(8,128)(2,1)S(1)}, u32[]{:S(2)}, u32[]{:S(2)}) %collective-permute-start.8) | collective-permute-done | bytes 196640 | tf_op jit(solution)/shard_map/ppermute | solution.py:415
  30.6 4.2 %collective-permute-done.6 = bf16[3,128,256]{2,1,0:T(8,128)(2,1)S(1)} collective-permute-done((bf16[3,128,256]{2,1,0:T(8,128)(2,1)S(1)}, bf16[3,128,256]{2,1,0:T(8,128)(2,1)S(1)}, u32[]{:S(2)}, u32[]{:S(2)}) %collective-permute-start.6) | collective-permute-done | bytes 196640 | tf_op jit(solution)/shard_map/ppermute | solution.py:415
  34.8 1.0 %pad_maximum_fusion.y0 = bf16[4,3,128,256]{3,2,1,0:T(8,128)(2,1)} fusion(bf16[1,3,128,256]{3,2,1,0:T(8,128)(2,1)S(1)} %bitcast.15, bf16[1,3,128,256]{3,2,1,0:T(8,128)(2,1)S(1)} %bitcast.14, bf16[1,3,128,256]{3,2,1,0:T(8,128)(2,1)S(1)} %bitcast.16, bf16[1,3,128,256]{3,2,1,0:T(8,128)(2,1)S(1)} %bitcast.12), kind=kLoop, calls=%fused_computation | loop fusion | flops 1179648 | bytes 1572864 | tf_op jit(solution)/shard_map/stack | solution.py:420
  35.8 2.8 %collective-permute-start.10 = (bf16[4,3,128,256]{3,2,1,0:T(8,128)(2,1)}, bf16[4,3,128,256]{3,2,1,0:T(8,128)(2,1)}, u32[]{:S(2)}, u32[]{:S(2)}) collective-permute-start(bf16[4,3,128,256]{3,2,1,0:T(8,128)(2,1)} %pad_maximum_fusion.y0), channel_id=1, source_target_pairs={{0,8},{1,9},{2,10},{3,11},{4,12},{5,13},{6,14},{7,15},{8,0},{9,1},... | collective-permute-start | bytes 2359304 | tf_op jit(solution)/shard_map/ppermute | solution.py:415
  38.6 1.0 %collective-permute-start.11 = (bf16[4,3,128,256]{3,2,1,0:T(8,128)(2,1)}, bf16[4,3,128,256]{3,2,1,0:T(8,128)(2,1)}, u32[]{:S(2)}, u32[]{:S(2)}) collective-permute-start(bf16[4,3,128,256]{3,2,1,0:T(8,128)(2,1)} %pad_maximum_fusion.y0), channel_id=1, source_target_pairs={{0,12},{1,13},{2,14},{3,15},{4,0},{5,1},{6,2},{7,3},{8,4},{9,5},{1... | collective-permute-start | bytes 2359304 | tf_op jit(solution)/shard_map/ppermute | solution.py:415
  39.6 1.0 %collective-permute-start.9 = (bf16[4,3,128,256]{3,2,1,0:T(8,128)(2,1)}, bf16[4,3,128,256]{3,2,1,0:T(8,128)(2,1)}, u32[]{:S(2)}, u32[]{:S(2)}) collective-permute-start(bf16[4,3,128,256]{3,2,1,0:T(8,128)(2,1)} %pad_maximum_fusion.y0), channel_id=1, source_target_pairs={{0,4},{1,5},{2,6},{3,7},{4,8},{5,9},{6,10},{7,11},{8,12},{9,13},{1... | collective-permute-start | bytes 2359304 | tf_op jit(solution)/shard_map/ppermute | solution.py:415
  40.6 38.7 %sinkhorn.1.p0 = f32[40,128]{1,0:T(8,128)S(1)} custom-call(s32[20]{0:T(128)S(1)} %get-tuple-element.14.params, f32[1]{0:T(128)S(6)} %copy.9.bins, bf16[4,2,128,256]{3,2,1,0:T(8,128)(2,1)S(1)} %pad_maximum_fusion.1.x0, bf16[4,2,128,256]{3,2,1,0:T(8,128)(2,1)S(1)} %collective-permute-done.3.x1, bf16[4,2,128,256]{3,2,1,0:T(8,128)(2,1)S(1)} %collective-permute-done.4.x2, ...), custom_call_target="tpu_custom_call" | custom-call | flops 199999995904 | bytes 2097152 | tf_op jit(solution)/shard_map/sinkhorn/pallas_call | solution.py:309
  79.4 0.1 collective-permute-start.12
  79.4 1.2 %collective-permute-start.13 = (f32[40,128]{1,0:T(8,128)S(1)}, f32[40,128]{1,0:T(8,128)S(1)}, u32[]{:S(2)}, u32[]{:S(2)}) collective-permute-start(f32[40,128]{1,0:T(8,128)S(1)} %sinkhorn.1.p0), channel_id=1, source_target_pairs={{0,2},{1,3},{2,0},{3,1},{4,6},{5,7},{6,4},{7,5},{8,10},{9,11},{10,... | collective-permute-start | bytes 61448 | tf_op jit(solution)/shard_map/ppermute | solution.py:423
  80.7 2.0 %collective-permute-start.14 = (f32[40,128]{1,0:T(8,128)S(1)}, f32[40,128]{1,0:T(8,128)S(1)}, u32[]{:S(2)}, u32[]{:S(2)}) collective-permute-start(f32[40,128]{1,0:T(8,128)S(1)} %sinkhorn.1.p0), channel_id=1, source_target_pairs={{0,3},{1,0},{2,1},{3,2},{4,7},{5,4},{6,5},{7,6},{8,11},{9,8},{10,9... | collective-permute-start | bytes 61448 | tf_op jit(solution)/shard_map/ppermute | solution.py:423
  82.7 3.6 %scores.1 = f32[4,128,2048]{2,1,0:T(8,128)S(1)} custom-call(s32[20]{0:T(128)S(1)} %get-tuple-element.14.params, bf16[8,128,256]{2,1,0:T(8,128)(2,1)S(1)} %copy-done.1, bf16[4,2,128,256]{3,2,1,0:T(8,128)(2,1)S(1)} %pad_maximum_fusion.1.x0, bf16[4,2,128,256]{3,2,1,0:T(8,128)(2,1)S(1)} %collective-permute-done.3.x1, ...), custom_call_target="tpu_custom_call" | custom-call | flops 8000000000 | bytes 8388608 | tf_op jit(solution)/shard_map/scores/pallas_call | solution.py:352
  86.3 0.0 collective-permute-done.14.p3
  86.3 3.7 %finish.1 = (f32[4,128,2048]{2,1,0:T(8,128)}, f32[4,128]{1,0:T(4,128)}, f32[4,2048]{1,0:T(4,128)}) custom-call(s32[20]{0:T(128)S(1)} %get-tuple-element.14.params, f32[1]{0:T(128)S(6)} %copy.9.bins, f32[4,128,2048]{2,1,0:T(8,128)S(1)} %scores.1, f32[40,128]{1,0:T(8,128)S(1)} %sinkhorn.1.p0, f32[40,128]{1,0:T(8,128)S(1)} %collective-permute-done.12.p1, ...), custom_call_target="tpu_custom_call" | custom-call | tf_op jit(solution)/shard_map/finish/pallas_call | solution.py:372
  (11 shorter events, 0.0 us)
Async XLA Ops:
  2.2 1.0 %copy-start = (bf16[8,128,256]{2,1,0:T(8,128)(2,1)S(1)}, bf16[8,128,256]{2,1,0:T(8,128)(2,1)}, u32[]{:S(2)}) copy-start(bf16[8,128,256]{2,1,0:T(8,128)(2,1)} %desc.2) | copy-start | bytes 1572868
  6.4 6.2 %collective-permute-start = (bf16[2,128,256]{2,1,0:T(8,128)(2,1)S(1)}, bf16[2,128,256]{2,1,0:T(8,128)(2,1)S(1)}, u32[]{:S(2)}, u32[]{:S(2)}) collective-permute-start(bf16[2,128,256]{2,1,0:T(8,128)(2,1)S(1)} %get-tuple-element.16), channel_id=1, source_target_pairs={{0,1},{1,2},{2,3},{3,0},{4,5},{5,6},{6,7},{7,4},{8,9},{9,10},{10,1... | collective-permute-start | bytes 393224 | tf_op jit(solution)/shard_map/ppermute | solution.py:415
  8.2 7.2 %collective-permute-start.1 = (bf16[2,128,256]{2,1,0:T(8,128)(2,1)S(1)}, bf16[2,128,256]{2,1,0:T(8,128)(2,1)S(1)}, u32[]{:S(2)}, u32[]{:S(2)}) collective-permute-start(bf16[2,128,256]{2,1,0:T(8,128)(2,1)S(1)} %get-tuple-element.17), channel_id=1, source_target_pairs={{0,2},{1,3},{2,0},{3,1},{4,6},{5,7},{6,4},{7,5},{8,10},{9,11},{10,... | collective-permute-start | bytes 393224 | tf_op jit(solution)/shard_map/ppermute | solution.py:415
  11.1 5.0 %collective-permute-start.2 = (bf16[2,128,256]{2,1,0:T(8,128)(2,1)S(1)}, bf16[2,128,256]{2,1,0:T(8,128)(2,1)S(1)}, u32[]{:S(2)}, u32[]{:S(2)}) collective-permute-start(bf16[2,128,256]{2,1,0:T(8,128)(2,1)S(1)} %get-tuple-element.18), channel_id=1, source_target_pairs={{0,3},{1,0},{2,1},{3,2},{4,7},{5,4},{6,5},{7,6},{8,11},{9,8},{10,9... | collective-permute-start | bytes 393224 | tf_op jit(solution)/shard_map/ppermute | solution.py:415
  12.5 12.8 %collective-permute-start.7 = (bf16[3,128,256]{2,1,0:T(8,128)(2,1)S(1)}, bf16[3,128,256]{2,1,0:T(8,128)(2,1)S(1)}, u32[]{:S(2)}, u32[]{:S(2)}) collective-permute-start(bf16[3,128,256]{2,1,0:T(8,128)(2,1)S(1)} %get-tuple-element.22), channel_id=1, source_target_pairs={{0,2},{1,3},{2,0},{3,1},{4,6},{5,7},{6,4},{7,5},{8,10},{9,11},{10,... | collective-permute-start | bytes 589832 | tf_op jit(solution)/shard_map/ppermute | solution.py:415
  16.1 23.5 %collective-permute-start.3 = (bf16[4,2,128,256]{3,2,1,0:T(8,128)(2,1)S(1)}, bf16[4,2,128,256]{3,2,1,0:T(8,128)(2,1)S(1)}, u32[]{:S(2)}, u32[]{:S(2)}) collective-permute-start(bf16[4,2,128,256]{3,2,1,0:T(8,128)(2,1)S(1)} %pad_maximum_fusion.1.x0), channel_id=1, source_target_pairs={{0,4},{1,5},{2,6},{3,7},{4,8},{5,9},{6,10},{7,11},{8,12},{9,13},{1... | collective-permute-start | bytes 1572872 | tf_op jit(solution)/shard_map/ppermute | solution.py:415
  18.1 22.5 %collective-permute-start.4 = (bf16[4,2,128,256]{3,2,1,0:T(8,128)(2,1)S(1)}, bf16[4,2,128,256]{3,2,1,0:T(8,128)(2,1)S(1)}, u32[]{:S(2)}, u32[]{:S(2)}) collective-permute-start(bf16[4,2,128,256]{3,2,1,0:T(8,128)(2,1)S(1)} %pad_maximum_fusion.1.x0), channel_id=1, source_target_pairs={{0,8},{1,9},{2,10},{3,11},{4,12},{5,13},{6,14},{7,15},{8,0},{9,1},... | collective-permute-start | bytes 1572872 | tf_op jit(solution)/shard_map/ppermute | solution.py:415
  21.7 18.9 %collective-permute-start.5 = (bf16[4,2,128,256]{3,2,1,0:T(8,128)(2,1)S(1)}, bf16[4,2,128,256]{3,2,1,0:T(8,128)(2,1)S(1)}, u32[]{:S(2)}, u32[]{:S(2)}) collective-permute-start(bf16[4,2,128,256]{3,2,1,0:T(8,128)(2,1)S(1)} %pad_maximum_fusion.1.x0), channel_id=1, source_target_pairs={{0,12},{1,13},{2,14},{3,15},{4,0},{5,1},{6,2},{7,3},{8,4},{9,5},{1... | collective-permute-start | bytes 1572872 | tf_op jit(solution)/shard_map/ppermute | solution.py:415
  22.7 7.9 %collective-permute-start.8 = (bf16[3,128,256]{2,1,0:T(8,128)(2,1)S(1)}, bf16[3,128,256]{2,1,0:T(8,128)(2,1)S(1)}, u32[]{:S(2)}, u32[]{:S(2)}) collective-permute-start(bf16[3,128,256]{2,1,0:T(8,128)(2,1)S(1)} %get-tuple-element.23), channel_id=1, source_target_pairs={{0,3},{1,0},{2,1},{3,2},{4,7},{5,4},{6,5},{7,6},{8,11},{9,8},{10,9... | collective-permute-start | bytes 589832 | tf_op jit(solution)/shard_map/ppermute | solution.py:415
  25.3 9.5 %collective-permute-start.6 = (bf16[3,128,256]{2,1,0:T(8,128)(2,1)S(1)}, bf16[3,128,256]{2,1,0:T(8,128)(2,1)S(1)}, u32[]{:S(2)}, u32[]{:S(2)}) collective-permute-start(bf16[3,128,256]{2,1,0:T(8,128)(2,1)S(1)} %get-tuple-element.21), channel_id=1, source_target_pairs={{0,1},{1,2},{2,3},{3,0},{4,5},{5,6},{6,7},{7,4},{8,9},{9,10},{10,1... | collective-permute-start | bytes 589832 | tf_op jit(solution)/shard_map/ppermute | solution.py:415
  35.8 44.9 %collective-permute-start.10 = (bf16[4,3,128,256]{3,2,1,0:T(8,128)(2,1)}, bf16[4,3,128,256]{3,2,1,0:T(8,128)(2,1)}, u32[]{:S(2)}, u32[]{:S(2)}) collective-permute-start(bf16[4,3,128,256]{3,2,1,0:T(8,128)(2,1)} %pad_maximum_fusion.y0), channel_id=1, source_target_pairs={{0,8},{1,9},{2,10},{3,11},{4,12},{5,13},{6,14},{7,15},{8,0},{9,1},... | collective-permute-start | bytes 2359304 | tf_op jit(solution)/shard_map/ppermute | solution.py:415
  38.6 44.1 %collective-permute-start.11 = (bf16[4,3,128,256]{3,2,1,0:T(8,128)(2,1)}, bf16[4,3,128,256]{3,2,1,0:T(8,128)(2,1)}, u32[]{:S(2)}, u32[]{:S(2)}) collective-permute-start(bf16[4,3,128,256]{3,2,1,0:T(8,128)(2,1)} %pad_maximum_fusion.y0), channel_id=1, source_target_pairs={{0,12},{1,13},{2,14},{3,15},{4,0},{5,1},{6,2},{7,3},{8,4},{9,5},{1... | collective-permute-start | bytes 2359304 | tf_op jit(solution)/shard_map/ppermute | solution.py:415
  39.6 43.0 %collective-permute-start.9 = (bf16[4,3,128,256]{3,2,1,0:T(8,128)(2,1)}, bf16[4,3,128,256]{3,2,1,0:T(8,128)(2,1)}, u32[]{:S(2)}, u32[]{:S(2)}) collective-permute-start(bf16[4,3,128,256]{3,2,1,0:T(8,128)(2,1)} %pad_maximum_fusion.y0), channel_id=1, source_target_pairs={{0,4},{1,5},{2,6},{3,7},{4,8},{5,9},{6,10},{7,11},{8,12},{9,13},{1... | collective-permute-start | bytes 2359304 | tf_op jit(solution)/shard_map/ppermute | solution.py:415
  40.6 42.1 %copy-start.1 = (bf16[8,128,256]{2,1,0:T(8,128)(2,1)S(1)}, bf16[8,128,256]{2,1,0:T(8,128)(2,1)}, u32[]{:S(2)}) copy-start(bf16[8,128,256]{2,1,0:T(8,128)(2,1)} %desc.2) | copy-start | bytes 1572868
  79.4 6.9 %collective-permute-start.12 = (f32[40,128]{1,0:T(8,128)S(1)}, f32[40,128]{1,0:T(8,128)S(1)}, u32[]{:S(2)}, u32[]{:S(2)}) collective-permute-start(f32[40,128]{1,0:T(8,128)S(1)} %sinkhorn.1.p0), channel_id=1, source_target_pairs={{0,1},{1,2},{2,3},{3,0},{4,5},{5,6},{6,7},{7,4},{8,9},{9,10},{10,1... | collective-permute-start | bytes 61448 | tf_op jit(solution)/shard_map/ppermute | solution.py:423
  79.4 6.8 %collective-permute-start.13 = (f32[40,128]{1,0:T(8,128)S(1)}, f32[40,128]{1,0:T(8,128)S(1)}, u32[]{:S(2)}, u32[]{:S(2)}) collective-permute-start(f32[40,128]{1,0:T(8,128)S(1)} %sinkhorn.1.p0), channel_id=1, source_target_pairs={{0,2},{1,3},{2,0},{3,1},{4,6},{5,7},{6,4},{7,5},{8,10},{9,11},{10,... | collective-permute-start | bytes 61448 | tf_op jit(solution)/shard_map/ppermute | solution.py:423
  80.7 5.6 %collective-permute-start.14 = (f32[40,128]{1,0:T(8,128)S(1)}, f32[40,128]{1,0:T(8,128)S(1)}, u32[]{:S(2)}, u32[]{:S(2)}) collective-permute-start(f32[40,128]{1,0:T(8,128)S(1)} %sinkhorn.1.p0), channel_id=1, source_target_pairs={{0,3},{1,0},{2,1},{3,2},{4,7},{5,4},{6,5},{7,6},{8,11},{9,8},{10,9... | collective-permute-start | bytes 61448 | tf_op jit(solution)/shard_map/ppermute | solution.py:423

commit v2 on v1

--- a/solution.py
+++ b/solution.py
@@ -289,9 +289,13 @@
             block[m, :, spot] = jnp.where(row_kept & col_kept, tile, 0.0)
             line = jnp.where(col_kept, alpha + pay[32:33, :] + col_pot - norm, 0.0)
             edges[c] = jnp.where(quarter == p, line, edges[c])
-        copy = pltpu.make_async_copy(block.at[m], match.at[p], sems.at[m])
-        copy.start()
-        stores.append(copy)
+            if c % 8 == 7:
+                half = pl.ds((c // 8) * (KP // 2), KP // 2)
+                copy = pltpu.make_async_copy(
+                    block.at[m, :, half], match.at[p, :, half], sems.at[m, c // 8]
+                )
+                copy.start()
+                stores.append(copy)
     row_bins[...] = side
     for c in range(NCH):
         col_bins[:, pl.ds(c * 128, 128)] = edges[c]
@@ -378,7 +382,7 @@
         ),
         in_specs=[SMEM()] * 2 + [VMEM()] * 5,
         out_specs=(ANY(), VMEM(), VMEM()),
-        scratch_shapes=[pltpu.VMEM((4, BLK, KP), f32), pltpu.SemaphoreType.DMA((4,))],
+        scratch_shapes=[pltpu.VMEM((4, BLK, KP), f32), pltpu.SemaphoreType.DMA((4, 2))],
         compiler_params=pltpu.CompilerParams(vmem_limit_bytes=16 * 1024 * 1024),
         name="finish",
     )(params, bins, scores, *pays)

time: 90.3 us -> 90.3 us (level)
  no operation moved by 1% of the time
where the time goes in v2:
time: 90.3 us; the launch traced here: 90.1 us
  Pallas kernels  49.1 us (54%)
  starting transfers between devices  23.5 us (26%)
  waiting for transfers between devices  12.3 us (14%)
  local copies, waits for them, and re-layouts  2.63 us (3%)
  between operations  1.55 us (2%)
  other arithmetic  1.05 us (1%)
    pallas_call x1, Pallas kernels, run_sinkhorn(): pl.pallas_call(sinkhorn_kernel, out_shape=jax.ShapeDtypeStruct((40, 128),...  38.7 us
    ppermute x12, starting transfers between devices, send(): arrived.append(lax.ppermute(x, AXES, moves(k)))  20.2 us
    ppermute x12, waiting for transfers between devices, send(): arrived.append(lax.ppermute(x, AXES, moves(k)))  12.3 us
    pallas_call x1, Pallas kernels, run_finish(): pl.pallas_call(finish_kernel, out_shape=(jax.ShapeDtypeStruct((4, BLK, KP...  3.67 us
    pallas_call x1, Pallas kernels, run_scores(): pl.pallas_call(score_kernel, out_shape=jax.ShapeDtypeStruct((4, BLK, KP),...  3.58 us
    ppermute x3, starting transfers between devices, on_device(): pays = [pay] + [lax.ppermute(pay, AXES, by_b(k)) for k in (1, 2, 3)]  3.3 us
    pallas_call x1, Pallas kernels, run_pick(): pl.pallas_call(pick_kernel, out_shape=(part,) * 4 + (more,) * 4 + (jax.Sh...  3.15 us
    unnamed x5, local copies, waits for them, and re-layouts  1.81 us
  transfers between devices with their start and end apart: 15, of which 4 were waited for; matrix products, arithmetic and copies ran while one was open for 1% of the time, Pallas kernels for 47%

profile of v2, /device:TPU:0, one launch (start us, length us, event | category | flops | bytes accessed | tf_op | source)
XLA Modules:
  0.0 90.1 jit_solution(4247893994618087123)
XLA Ops:
  0.7 0.8 copy.8
  1.4 0.1 reshape.9
  1.5 0.7 concatenate.3.index
  2.2 1.0 %copy-done = bf16[8,128,256]{2,1,0:T(8,128)(2,1)S(1)} copy-done((bf16[8,128,256]{2,1,0:T(8,128)(2,1)S(1)}, bf16[8,128,256]{2,1,0:T(8,128)(2,1)}, u32[]{:S(2)}) %copy-start) | copy-done | bytes 524312
  3.3 3.2 %pick.1 = (bf16[2,128,256]{2,1,0:T(8,128)(2,1)S(1)}, bf16[2,128,256]{2,1,0:T(8,128)(2,1)S(1)}, bf16[2,128,256]{2,1,0:T(8,128)(2,1)S(1)}, bf16[2,128,256]{2,1,0:T...) custom-call(s32[20]{0:T(128)S(1)} %concatenate.3.index, ...), custom_call_target="tpu_custom_call" | custom-call | tf_op jit(solution)/shard_map/pick/pallas_call | solution.py:344
  6.4 1.8 %collective-permute-start = (bf16[2,128,256]{2,1,0:T(8,128)(2,1)S(1)}, bf16[2,128,256]{2,1,0:T(8,128)(2,1)S(1)}, u32[]{:S(2)}, u32[]{:S(2)}) collective-permute-start(bf16[2,128,256]{2,1,0:T(8,128)(2,1)S(1)} %get-tuple-element.16), channel_id=1, source_target_pairs={{0,1},{1,2},{2,3},{3,0},{4,5},{5,6},{6,7},{7,4},{8,9},{9,10},{10,1... | collective-permute-start | bytes 393224 | tf_op jit(solution)/shard_map/ppermute | solution.py:419
  8.2 2.9 %collective-permute-start.1 = (bf16[2,128,256]{2,1,0:T(8,128)(2,1)S(1)}, bf16[2,128,256]{2,1,0:T(8,128)(2,1)S(1)}, u32[]{:S(2)}, u32[]{:S(2)}) collective-permute-start(bf16[2,128,256]{2,1,0:T(8,128)(2,1)S(1)} %get-tuple-element.17), channel_id=1, source_target_pairs={{0,2},{1,3},{2,0},{3,1},{4,6},{5,7},{6,4},{7,5},{8,10},{9,11},{10,... | collective-permute-start | bytes 393224 | tf_op jit(solution)/shard_map/ppermute | solution.py:419
  11.1 1.3 %collective-permute-start.2 = (bf16[2,128,256]{2,1,0:T(8,128)(2,1)S(1)}, bf16[2,128,256]{2,1,0:T(8,128)(2,1)S(1)}, u32[]{:S(2)}, u32[]{:S(2)}) collective-permute-start(bf16[2,128,256]{2,1,0:T(8,128)(2,1)S(1)} %get-tuple-element.18), channel_id=1, source_target_pairs={{0,3},{1,0},{2,1},{3,2},{4,7},{5,4},{6,5},{7,6},{8,11},{9,8},{10,9... | collective-permute-start | bytes 393224 | tf_op jit(solution)/shard_map/ppermute | solution.py:419
  12.5 0.2 collective-permute-start.7
  12.7 0.0 collective-permute-done
  12.7 2.8 %collective-permute-done.1 = bf16[2,128,256]{2,1,0:T(8,128)(2,1)S(1)} collective-permute-done((bf16[2,128,256]{2,1,0:T(8,128)(2,1)S(1)}, bf16[2,128,256]{2,1,0:T(8,128)(2,1)S(1)}, u32[]{:S(2)}, u32[]{:S(2)}) %collective-permute-start.1) | collective-permute-done | bytes 131104 | tf_op jit(solution)/shard_map/ppermute | solution.py:419
  15.4 0.6 collective-permute-done.2
  16.1 0.1 pad_maximum_fusion.1.x0
  16.1 2.0 %collective-permute-start.3 = (bf16[4,2,128,256]{3,2,1,0:T(8,128)(2,1)S(1)}, bf16[4,2,128,256]{3,2,1,0:T(8,128)(2,1)S(1)}, u32[]{:S(2)}, u32[]{:S(2)}) collective-permute-start(bf16[4,2,128,256]{3,2,1,0:T(8,128)(2,1)S(1)} %pad_maximum_fusion.1.x0), channel_id=1, source_target_pairs={{0,4},{1,5},{2,6},{3,7},{4,8},{5,9},{6,10},{7,11},{8,12},{9,13},{1... | collective-permute-start | bytes 1572872 | tf_op jit(solution)/shard_map/ppermute | solution.py:419
  18.1 3.6 %collective-permute-start.4 = (bf16[4,2,128,256]{3,2,1,0:T(8,128)(2,1)S(1)}, bf16[4,2,128,256]{3,2,1,0:T(8,128)(2,1)S(1)}, u32[]{:S(2)}, u32[]{:S(2)}) collective-permute-start(bf16[4,2,128,256]{3,2,1,0:T(8,128)(2,1)S(1)} %pad_maximum_fusion.1.x0), channel_id=1, source_target_pairs={{0,8},{1,9},{2,10},{3,11},{4,12},{5,13},{6,14},{7,15},{8,0},{9,1},... | collective-permute-start | bytes 1572872 | tf_op jit(solution)/shard_map/ppermute | solution.py:419
  21.7 1.0 %collective-permute-start.5 = (bf16[4,2,128,256]{3,2,1,0:T(8,128)(2,1)S(1)}, bf16[4,2,128,256]{3,2,1,0:T(8,128)(2,1)S(1)}, u32[]{:S(2)}, u32[]{:S(2)}) collective-permute-start(bf16[4,2,128,256]{3,2,1,0:T(8,128)(2,1)S(1)} %pad_maximum_fusion.1.x0), channel_id=1, source_target_pairs={{0,12},{1,13},{2,14},{3,15},{4,0},{5,1},{6,2},{7,3},{8,4},{9,5},{1... | collective-permute-start | bytes 1572872 | tf_op jit(solution)/shard_map/ppermute | solution.py:419
  22.7 2.6 %collective-permute-start.8 = (bf16[3,128,256]{2,1,0:T(8,128)(2,1)S(1)}, bf16[3,128,256]{2,1,0:T(8,128)(2,1)S(1)}, u32[]{:S(2)}, u32[]{:S(2)}) collective-permute-start(bf16[3,128,256]{2,1,0:T(8,128)(2,1)S(1)} %get-tuple-element.23), channel_id=1, source_target_pairs={{0,3},{1,0},{2,1},{3,2},{4,7},{5,4},{6,5},{7,6},{8,11},{9,8},{10,9... | collective-permute-start | bytes 589832 | tf_op jit(solution)/shard_map/ppermute | solution.py:419
  25.3 0.0 collective-permute-done.7
  25.3 0.0 collective-permute-start.6
  25.9 4.6 %collective-permute-done.8 = bf16[3,128,256]{2,1,0:T(8,128)(2,1)S(1)} collective-permute-done((bf16[3,128,256]{2,1,0:T(8,128)(2,1)S(1)}, bf16[3,128,256]{2,1,0:T(8,128)(2,1)S(1)}, u32[]{:S(2)}, u32[]{:S(2)}) %collective-permute-start.8) | collective-permute-done | bytes 196640 | tf_op jit(solution)/shard_map/ppermute | solution.py:419
  30.6 4.2 %collective-permute-done.6 = bf16[3,128,256]{2,1,0:T(8,128)(2,1)S(1)} collective-permute-done((bf16[3,128,256]{2,1,0:T(8,128)(2,1)S(1)}, bf16[3,128,256]{2,1,0:T(8,128)(2,1)S(1)}, u32[]{:S(2)}, u32[]{:S(2)}) %collective-permute-start.6) | collective-permute-done | bytes 196640 | tf_op jit(solution)/shard_map/ppermute | solution.py:419
  34.8 1.0 %pad_maximum_fusion.y0 = bf16[4,3,128,256]{3,2,1,0:T(8,128)(2,1)} fusion(bf16[1,3,128,256]{3,2,1,0:T(8,128)(2,1)S(1)} %bitcast.15, bf16[1,3,128,256]{3,2,1,0:T(8,128)(2,1)S(1)} %bitcast.14, bf16[1,3,128,256]{3,2,1,0:T(8,128)(2,1)S(1)} %bitcast.16, bf16[1,3,128,256]{3,2,1,0:T(8,128)(2,1)S(1)} %bitcast.12), kind=kLoop, calls=%fused_computation | loop fusion | flops 1179648 | bytes 1572864 | tf_op jit(solution)/shard_map/stack | solution.py:424
  35.8 2.8 %collective-permute-start.10 = (bf16[4,3,128,256]{3,2,1,0:T(8,128)(2,1)}, bf16[4,3,128,256]{3,2,1,0:T(8,128)(2,1)}, u32[]{:S(2)}, u32[]{:S(2)}) collective-permute-start(bf16[4,3,128,256]{3,2,1,0:T(8,128)(2,1)} %pad_maximum_fusion.y0), channel_id=1, source_target_pairs={{0,8},{1,9},{2,10},{3,11},{4,12},{5,13},{6,14},{7,15},{8,0},{9,1},... | collective-permute-start | bytes 2359304 | tf_op jit(solution)/shard_map/ppermute | solution.py:419
  38.6 1.0 %collective-permute-start.11 = (bf16[4,3,128,256]{3,2,1,0:T(8,128)(2,1)}, bf16[4,3,128,256]{3,2,1,0:T(8,128)(2,1)}, u32[]{:S(2)}, u32[]{:S(2)}) collective-permute-start(bf16[4,3,128,256]{3,2,1,0:T(8,128)(2,1)} %pad_maximum_fusion.y0), channel_id=1, source_target_pairs={{0,12},{1,13},{2,14},{3,15},{4,0},{5,1},{6,2},{7,3},{8,4},{9,5},{1... | collective-permute-start | bytes 2359304 | tf_op jit(solution)/shard_map/ppermute | solution.py:419
  39.6 1.0 %collective-permute-start.9 = (bf16[4,3,128,256]{3,2,1,0:T(8,128)(2,1)}, bf16[4,3,128,256]{3,2,1,0:T(8,128)(2,1)}, u32[]{:S(2)}, u32[]{:S(2)}) collective-permute-start(bf16[4,3,128,256]{3,2,1,0:T(8,128)(2,1)} %pad_maximum_fusion.y0), channel_id=1, source_target_pairs={{0,4},{1,5},{2,6},{3,7},{4,8},{5,9},{6,10},{7,11},{8,12},{9,13},{1... | collective-permute-start | bytes 2359304 | tf_op jit(solution)/shard_map/ppermute | solution.py:419
  40.6 38.7 %sinkhorn.1.p0 = f32[40,128]{1,0:T(8,128)S(1)} custom-call(s32[20]{0:T(128)S(1)} %get-tuple-element.14.params, f32[1]{0:T(128)S(6)} %copy.9.bins, bf16[4,2,128,256]{3,2,1,0:T(8,128)(2,1)S(1)} %pad_maximum_fusion.1.x0, bf16[4,2,128,256]{3,2,1,0:T(8,128)(2,1)S(1)} %collective-permute-done.3.x1, bf16[4,2,128,256]{3,2,1,0:T(8,128)(2,1)S(1)} %collective-permute-done.4.x2, ...), custom_call_target="tpu_custom_call" | custom-call | flops 199999995904 | bytes 2097152 | tf_op jit(solution)/shard_map/sinkhorn/pallas_call | solution.py:313
  79.4 0.1 collective-permute-start.12
  79.4 1.2 %collective-permute-start.13 = (f32[40,128]{1,0:T(8,128)S(1)}, f32[40,128]{1,0:T(8,128)S(1)}, u32[]{:S(2)}, u32[]{:S(2)}) collective-permute-start(f32[40,128]{1,0:T(8,128)S(1)} %sinkhorn.1.p0), channel_id=1, source_target_pairs={{0,2},{1,3},{2,0},{3,1},{4,6},{5,7},{6,4},{7,5},{8,10},{9,11},{10,... | collective-permute-start | bytes 61448 | tf_op jit(solution)/shard_map/ppermute | solution.py:427
  80.7 2.0 %collective-permute-start.14 = (f32[40,128]{1,0:T(8,128)S(1)}, f32[40,128]{1,0:T(8,128)S(1)}, u32[]{:S(2)}, u32[]{:S(2)}) collective-permute-start(f32[40,128]{1,0:T(8,128)S(1)} %sinkhorn.1.p0), channel_id=1, source_target_pairs={{0,3},{1,0},{2,1},{3,2},{4,7},{5,4},{6,5},{7,6},{8,11},{9,8},{10,9... | collective-permute-start | bytes 61448 | tf_op jit(solution)/shard_map/ppermute | solution.py:427
  82.7 3.6 %scores.1 = f32[4,128,2048]{2,1,0:T(8,128)S(1)} custom-call(s32[20]{0:T(128)S(1)} %get-tuple-element.14.params, bf16[8,128,256]{2,1,0:T(8,128)(2,1)S(1)} %copy-done.1, bf16[4,2,128,256]{3,2,1,0:T(8,128)(2,1)S(1)} %pad_maximum_fusion.1.x0, bf16[4,2,128,256]{3,2,1,0:T(8,128)(2,1)S(1)} %collective-permute-done.3.x1, ...), custom_call_target="tpu_custom_call" | custom-call | flops 8000000000 | bytes 8388608 | tf_op jit(solution)/shard_map/scores/pallas_call | solution.py:356
  86.3 0.0 collective-permute-done.14.p3
  86.3 3.7 %finish.1 = (f32[4,128,2048]{2,1,0:T(8,128)}, f32[4,128]{1,0:T(4,128)}, f32[4,2048]{1,0:T(4,128)}) custom-call(s32[20]{0:T(128)S(1)} %get-tuple-element.14.params, f32[1]{0:T(128)S(6)} %copy.9.bins, f32[4,128,2048]{2,1,0:T(8,128)S(1)} %scores.1, f32[40,128]{1,0:T(8,128)S(1)} %sinkhorn.1.p0, f32[40,128]{1,0:T(8,128)S(1)} %collective-permute-done.12.p1, ...), custom_call_target="tpu_custom_call" | custom-call | tf_op jit(solution)/shard_map/finish/pallas_call | solution.py:376
  (11 shorter events, 0.0 us)
Async XLA Ops:
  2.2 1.0 %copy-start = (bf16[8,128,256]{2,1,0:T(8,128)(2,1)S(1)}, bf16[8,128,256]{2,1,0:T(8,128)(2,1)}, u32[]{:S(2)}) copy-start(bf16[8,128,256]{2,1,0:T(8,128)(2,1)} %desc.2) | copy-start | bytes 1572868
  6.4 6.2 %collective-permute-start = (bf16[2,128,256]{2,1,0:T(8,128)(2,1)S(1)}, bf16[2,128,256]{2,1,0:T(8,128)(2,1)S(1)}, u32[]{:S(2)}, u32[]{:S(2)}) collective-permute-start(bf16[2,128,256]{2,1,0:T(8,128)(2,1)S(1)} %get-tuple-element.16), channel_id=1, source_target_pairs={{0,1},{1,2},{2,3},{3,0},{4,5},{5,6},{6,7},{7,4},{8,9},{9,10},{10,1... | collective-permute-start | bytes 393224 | tf_op jit(solution)/shard_map/ppermute | solution.py:419
  8.2 7.2 %collective-permute-start.1 = (bf16[2,128,256]{2,1,0:T(8,128)(2,1)S(1)}, bf16[2,128,256]{2,1,0:T(8,128)(2,1)S(1)}, u32[]{:S(2)}, u32[]{:S(2)}) collective-permute-start(bf16[2,128,256]{2,1,0:T(8,128)(2,1)S(1)} %get-tuple-element.17), channel_id=1, source_target_pairs={{0,2},{1,3},{2,0},{3,1},{4,6},{5,7},{6,4},{7,5},{8,10},{9,11},{10,... | collective-permute-start | bytes 393224 | tf_op jit(solution)/shard_map/ppermute | solution.py:419
  11.1 5.0 %collective-permute-start.2 = (bf16[2,128,256]{2,1,0:T(8,128)(2,1)S(1)}, bf16[2,128,256]{2,1,0:T(8,128)(2,1)S(1)}, u32[]{:S(2)}, u32[]{:S(2)}) collective-permute-start(bf16[2,128,256]{2,1,0:T(8,128)(2,1)S(1)} %get-tuple-element.18), channel_id=1, source_target_pairs={{0,3},{1,0},{2,1},{3,2},{4,7},{5,4},{6,5},{7,6},{8,11},{9,8},{10,9... | collective-permute-start | bytes 393224 | tf_op jit(solution)/shard_map/ppermute | solution.py:419
  12.5 12.8 %collective-permute-start.7 = (bf16[3,128,256]{2,1,0:T(8,128)(2,1)S(1)}, bf16[3,128,256]{2,1,0:T(8,128)(2,1)S(1)}, u32[]{:S(2)}, u32[]{:S(2)}) collective-permute-start(bf16[3,128,256]{2,1,0:T(8,128)(2,1)S(1)} %get-tuple-element.22), channel_id=1, source_target_pairs={{0,2},{1,3},{2,0},{3,1},{4,6},{5,7},{6,4},{7,5},{8,10},{9,11},{10,... | collective-permute-start | bytes 589832 | tf_op jit(solution)/shard_map/ppermute | solution.py:419
  16.1 23.5 %collective-permute-start.3 = (bf16[4,2,128,256]{3,2,1,0:T(8,128)(2,1)S(1)}, bf16[4,2,128,256]{3,2,1,0:T(8,128)(2,1)S(1)}, u32[]{:S(2)}, u32[]{:S(2)}) collective-permute-start(bf16[4,2,128,256]{3,2,1,0:T(8,128)(2,1)S(1)} %pad_maximum_fusion.1.x0), channel_id=1, source_target_pairs={{0,4},{1,5},{2,6},{3,7},{4,8},{5,9},{6,10},{7,11},{8,12},{9,13},{1... | collective-permute-start | bytes 1572872 | tf_op jit(solution)/shard_map/ppermute | solution.py:419
  18.1 22.5 %collective-permute-start.4 = (bf16[4,2,128,256]{3,2,1,0:T(8,128)(2,1)S(1)}, bf16[4,2,128,256]{3,2,1,0:T(8,128)(2,1)S(1)}, u32[]{:S(2)}, u32[]{:S(2)}) collective-permute-start(bf16[4,2,128,256]{3,2,1,0:T(8,128)(2,1)S(1)} %pad_maximum_fusion.1.x0), channel_id=1, source_target_pairs={{0,8},{1,9},{2,10},{3,11},{4,12},{5,13},{6,14},{7,15},{8,0},{9,1},... | collective-permute-start | bytes 1572872 | tf_op jit(solution)/shard_map/ppermute | solution.py:419
  21.7 18.9 %collective-permute-start.5 = (bf16[4,2,128,256]{3,2,1,0:T(8,128)(2,1)S(1)}, bf16[4,2,128,256]{3,2,1,0:T(8,128)(2,1)S(1)}, u32[]{:S(2)}, u32[]{:S(2)}) collective-permute-start(bf16[4,2,128,256]{3,2,1,0:T(8,128)(2,1)S(1)} %pad_maximum_fusion.1.x0), channel_id=1, source_target_pairs={{0,12},{1,13},{2,14},{3,15},{4,0},{5,1},{6,2},{7,3},{8,4},{9,5},{1... | collective-permute-start | bytes 1572872 | tf_op jit(solution)/shard_map/ppermute | solution.py:419
  22.7 7.9 %collective-permute-start.8 = (bf16[3,128,256]{2,1,0:T(8,128)(2,1)S(1)}, bf16[3,128,256]{2,1,0:T(8,128)(2,1)S(1)}, u32[]{:S(2)}, u32[]{:S(2)}) collective-permute-start(bf16[3,128,256]{2,1,0:T(8,128)(2,1)S(1)} %get-tuple-element.23), channel_id=1, source_target_pairs={{0,3},{1,0},{2,1},{3,2},{4,7},{5,4},{6,5},{7,6},{8,11},{9,8},{10,9... | collective-permute-start | bytes 589832 | tf_op jit(solution)/shard_map/ppermute | solution.py:419
  25.3 9.5 %collective-permute-start.6 = (bf16[3,128,256]{2,1,0:T(8,128)(2,1)S(1)}, bf16[3,128,256]{2,1,0:T(8,128)(2,1)S(1)}, u32[]{:S(2)}, u32[]{:S(2)}) collective-permute-start(bf16[3,128,256]{2,1,0:T(8,128)(2,1)S(1)} %get-tuple-element.21), channel_id=1, source_target_pairs={{0,1},{1,2},{2,3},{3,0},{4,5},{5,6},{6,7},{7,4},{8,9},{9,10},{10,1... | collective-permute-start | bytes 589832 | tf_op jit(solution)/shard_map/ppermute | solution.py:419
  35.8 44.9 %collective-permute-start.10 = (bf16[4,3,128,256]{3,2,1,0:T(8,128)(2,1)}, bf16[4,3,128,256]{3,2,1,0:T(8,128)(2,1)}, u32[]{:S(2)}, u32[]{:S(2)}) collective-permute-start(bf16[4,3,128,256]{3,2,1,0:T(8,128)(2,1)} %pad_maximum_fusion.y0), channel_id=1, source_target_pairs={{0,8},{1,9},{2,10},{3,11},{4,12},{5,13},{6,14},{7,15},{8,0},{9,1},... | collective-permute-start | bytes 2359304 | tf_op jit(solution)/shard_map/ppermute | solution.py:419
  38.6 44.1 %collective-permute-start.11 = (bf16[4,3,128,256]{3,2,1,0:T(8,128)(2,1)}, bf16[4,3,128,256]{3,2,1,0:T(8,128)(2,1)}, u32[]{:S(2)}, u32[]{:S(2)}) collective-permute-start(bf16[4,3,128,256]{3,2,1,0:T(8,128)(2,1)} %pad_maximum_fusion.y0), channel_id=1, source_target_pairs={{0,12},{1,13},{2,14},{3,15},{4,0},{5,1},{6,2},{7,3},{8,4},{9,5},{1... | collective-permute-start | bytes 2359304 | tf_op jit(solution)/shard_map/ppermute | solution.py:419
  39.6 43.0 %collective-permute-start.9 = (bf16[4,3,128,256]{3,2,1,0:T(8,128)(2,1)}, bf16[4,3,128,256]{3,2,1,0:T(8,128)(2,1)}, u32[]{:S(2)}, u32[]{:S(2)}) collective-permute-start(bf16[4,3,128,256]{3,2,1,0:T(8,128)(2,1)} %pad_maximum_fusion.y0), channel_id=1, source_target_pairs={{0,4},{1,5},{2,6},{3,7},{4,8},{5,9},{6,10},{7,11},{8,12},{9,13},{1... | collective-permute-start | bytes 2359304 | tf_op jit(solution)/shard_map/ppermute | solution.py:419
  40.6 42.1 %copy-start.1 = (bf16[8,128,256]{2,1,0:T(8,128)(2,1)S(1)}, bf16[8,128,256]{2,1,0:T(8,128)(2,1)}, u32[]{:S(2)}) copy-start(bf16[8,128,256]{2,1,0:T(8,128)(2,1)} %desc.2) | copy-start | bytes 1572868
  79.4 6.9 %collective-permute-start.12 = (f32[40,128]{1,0:T(8,128)S(1)}, f32[40,128]{1,0:T(8,128)S(1)}, u32[]{:S(2)}, u32[]{:S(2)}) collective-permute-start(f32[40,128]{1,0:T(8,128)S(1)} %sinkhorn.1.p0), channel_id=1, source_target_pairs={{0,1},{1,2},{2,3},{3,0},{4,5},{5,6},{6,7},{7,4},{8,9},{9,10},{10,1... | collective-permute-start | bytes 61448 | tf_op jit(solution)/shard_map/ppermute | solution.py:427
  79.4 6.8 %collective-permute-start.13 = (f32[40,128]{1,0:T(8,128)S(1)}, f32[40,128]{1,0:T(8,128)S(1)}, u32[]{:S(2)}, u32[]{:S(2)}) collective-permute-start(f32[40,128]{1,0:T(8,128)S(1)} %sinkhorn.1.p0), channel_id=1, source_target_pairs={{0,2},{1,3},{2,0},{3,1},{4,6},{5,7},{6,4},{7,5},{8,10},{9,11},{10,... | collective-permute-start | bytes 61448 | tf_op jit(solution)/shard_map/ppermute | solution.py:427
  80.7 5.6 %collective-permute-start.14 = (f32[40,128]{1,0:T(8,128)S(1)}, f32[40,128]{1,0:T(8,128)S(1)}, u32[]{:S(2)}, u32[]{:S(2)}) collective-permute-start(f32[40,128]{1,0:T(8,128)S(1)} %sinkhorn.1.p0), channel_id=1, source_target_pairs={{0,3},{1,0},{2,1},{3,2},{4,7},{5,4},{6,5},{7,6},{8,11},{9,8},{10,9... | collective-permute-start | bytes 61448 | tf_op jit(solution)/shard_map/ppermute | solution.py:427
